TPU v7x, 32 devices: a whole 2x2x4 slice. The times are simulated.
32 devices in a mesh: dp: 8 (over z, x), mp: 4 (over y, core).
Axes of the slice: x: 2, y: 2, z: 4, core: 2. Of those that a mesh axis runs over, the one named last changes fastest.
Arguments:
- tokens: bfloat16 [16384, 1024], P(('dp', 'mp')), may hold values from -6 to 6
- lengths: int32 [8, 1], P('dp'), may hold values from 30 to 2048, as said below
- query_weight: bfloat16 [1024, 1024], P(None, 'mp'), may hold values from -0.25 to 0.25
- query_bias: bfloat16 [1024], P('mp'), may hold values from -3 to 3
- key_weight: bfloat16 [1024, 1024], P(None, 'mp'), may hold values from -0.25 to 0.25
- value_weight: bfloat16 [1024, 1024], P(None, 'mp'), may hold values from -0.1875 to 0.1875
- value_bias: bfloat16 [1024], P('mp'), may hold values from -3 to 3
- out_weight: bfloat16 [1024, 1024], P('mp'), may hold values from -0.75 to 0.75
- out_bias: bfloat16 [1024], replicated, may hold values from -3 to 3
- first_gain: bfloat16 [1024], replicated, may hold values from 0.25 to 1.75
- first_shift: bfloat16 [1024], replicated, may hold values from -3 to 3
- up_weight: bfloat16 [1024, 4096], P(None, 'mp'), may hold values from -0.1875 to 0.1875
- up_bias: bfloat16 [4096], P('mp'), may hold values from -3 to 3
- down_weight: bfloat16 [4096, 1024], P('mp'), may hold values from -0.09375 to 0.09375
- down_bias: bfloat16 [1024], replicated, may hold values from -3 to 3
- second_gain: bfloat16 [1024], replicated, may hold values from 0.25 to 1.75
- second_shift: bfloat16 [1024], replicated, may hold values from -3 to 3
- output_grad: bfloat16 [16384, 1024], P(('dp', 'mp')), may hold values from -6 to 6
Outputs:
- layer_out: bfloat16 [16384, 1024], P(('dp', 'mp'))
- tokens_grad: bfloat16 [16384, 1024], P(('dp', 'mp'))
- query_weight_grad: float32 [1024, 1024], P(None, 'mp')
- query_bias_grad: float32 [1024], P('mp')
- key_weight_grad: float32 [1024, 1024], P(None, 'mp')
- value_weight_grad: float32 [1024, 1024], P(None, 'mp')
- value_bias_grad: float32 [1024], P('mp')
- out_weight_grad: float32 [1024, 1024], P('mp')
- out_bias_grad: float32 [1024], replicated
- first_gain_grad: float32 [1024], replicated
- first_shift_grad: float32 [1024], replicated
- up_weight_grad: float32 [1024, 4096], P(None, 'mp')
- up_bias_grad: float32 [4096], P('mp')
- down_weight_grad: float32 [4096, 1024], P('mp')
- down_bias_grad: float32 [1024], replicated
- second_gain_grad: float32 [1024], replicated
- second_shift_grad: float32 [1024], replicated
Inputs may be any that keep to these rules, and one draw needn't show every extreme that they name: Batch b holds 1 sequence of 2048 rows; sequence s counts its first lengths[b, s] rows as keys; in every draw some sequence has exactly 2048.
All inputs are finite; a program needn't handle non-finite values.
Results may differ from a plain program's by a relative error of at most 0.023.
Values may be sent and summed in bfloat16 or wider, within the bound.
A program may use at most 320 MiB of HBM per device.

v0:
```python
from functools import partial

import jax
import jax.numpy as jnp
from jax import lax
from jax.sharding import PartitionSpec as P

HD = 64


epsilon = 1e-12


def norm_forward(resid, gain, shift):
    center = resid - jnp.mean(resid, -1, keepdims=True)
    inv_std = lax.rsqrt(jnp.mean(center * center, -1, keepdims=True) + epsilon)
    normed = center * inv_std
    return (normed * gain + shift, normed, inv_std)


def norm_backward(grad, normed, inv_std, gain):
    scaled = grad * gain
    back = inv_std * (
        scaled
        - jnp.mean(scaled, -1, keepdims=True)
        - normed * jnp.mean(scaled * normed, -1, keepdims=True)
    )
    return (back, jnp.sum(grad * normed, 0), jnp.sum(grad, 0))


def masked_scores(query_blk, key_rows, length):
    scores = jnp.einsum(
        "qhd,khd->hqk", query_blk, key_rows, preferred_element_type=jnp.float32
    ) * HD ** (-0.5)
    valid = lax.iota(jnp.int32, key_rows.shape[0]) < length
    return jnp.where(valid[None, None, :], scores, -1000000000.0)


def sequence_forward(carried, inputs):
    queries, key_rows, values, length = inputs
    seq_len = queries.shape[0]
    block_rows = min(512, seq_len)
    outputs = []
    log_sums = []
    for offset in range(0, seq_len, block_rows):
        scores = masked_scores(queries[offset : offset + block_rows], key_rows, length)
        row_max = jnp.max(scores, -1, keepdims=True)
        expon = jnp.exp(scores - row_max)
        row_sum = jnp.sum(expon, -1, keepdims=True)
        probs = (expon / row_sum).astype(jnp.bfloat16)
        outputs.append(
            jnp.einsum("hqk,khd->qhd", probs, values, preferred_element_type=jnp.float32)
        )
        log_sums.append((row_max + jnp.log(row_sum))[..., 0])
    return (carried, (jnp.concatenate(outputs, 0), jnp.concatenate(log_sums, 1)))


def sequence_backward(carried, inputs):
    queries, key_rows, values, out_grad, log_sums, length = inputs
    seq_len = queries.shape[0]
    block_rows = min(512, seq_len)
    scale = HD ** (-0.5)
    key_grad = jnp.zeros(key_rows.shape, jnp.float32)
    value_grad = jnp.zeros(values.shape, jnp.float32)
    query_grads = []
    for offset in range(0, seq_len, block_rows):
        query_blk = queries[offset : offset + block_rows]
        grad_blk = out_grad[offset : offset + block_rows]
        scores = masked_scores(query_blk, key_rows, length)
        probs = jnp.exp(scores - log_sums[:, offset : offset + block_rows, None])
        value_grad = value_grad + jnp.einsum(
            "hqk,qhd->khd", probs.astype(jnp.bfloat16), grad_blk, preferred_element_type=jnp.float32
        )
        prob_grad = jnp.einsum("qhd,khd->hqk", grad_blk, values, preferred_element_type=jnp.float32)
        score_grad = (probs * (prob_grad - jnp.sum(probs * prob_grad, -1, keepdims=True))).astype(
            jnp.bfloat16
        )
        query_grads.append(
            (
                jnp.einsum("hqk,khd->qhd", score_grad, key_rows, preferred_element_type=jnp.float32)
                * scale
            ).astype(jnp.bfloat16)
        )
        key_grad = (
            key_grad
            + jnp.einsum("hqk,qhd->khd", score_grad, query_blk, preferred_element_type=jnp.float32)
            * scale
        )
    return (
        carried,
        (
            jnp.concatenate(query_grads, 0),
            key_grad.astype(jnp.bfloat16),
            value_grad.astype(jnp.bfloat16),
        ),
    )


def contract_rows(left, right):
    return lax.dot_general(
        left, right, (((0,), (0,)), ((), ())), preferred_element_type=jnp.float32
    )


def contract_cols(left, right):
    return lax.dot_general(
        left, right, (((1,), (1,)), ((), ())), preferred_element_type=jnp.float32
    )


def split_projection(projected, width, q_bias, v_bias):
    query_part = (projected[:, :width] + q_bias).astype(jnp.bfloat16)
    key_part = projected[:, width : 2 * width].astype(jnp.bfloat16)
    value_part = (projected[:, 2 * width :] + v_bias).astype(jnp.bfloat16)
    return (query_part, key_part, value_part)


def per_device(
    tokens,
    lengths,
    query_weight,
    query_bias,
    key_weight,
    value_weight,
    value_bias,
    out_weight,
    out_bias,
    first_gain,
    first_shift,
    up_weight,
    up_bias,
    down_weight,
    down_bias,
    second_gain,
    second_shift,
    output_grad,
):
    local_rows = tokens.shape[0]
    head_cols = query_weight.shape[1]
    heads_here = head_cols // HD
    seq_count = lengths.shape[1]
    all_rows = local_rows * lax.axis_size("mp")
    seq_len = all_rows // seq_count
    shape4 = (seq_count, seq_len, heads_here, HD)
    gathered = lax.all_gather(tokens, "mp", axis=0, tiled=True)
    joint_weight = jnp.concatenate([query_weight, key_weight, value_weight], 1)
    projected = jnp.dot(gathered, joint_weight, preferred_element_type=jnp.float32)
    queries, key_rows, values = split_projection(projected, head_cols, query_bias, value_bias)
    queries = queries.reshape(shape4)
    key_rows = key_rows.reshape(shape4)
    values = values.reshape(shape4)
    unused_one, (attended, log_sums) = lax.scan(
        sequence_forward, 0, (queries, key_rows, values, lengths[0])
    )
    attended = attended.reshape(all_rows, head_cols).astype(jnp.bfloat16)
    branch_one = lax.psum_scatter(
        jnp.dot(
            lax.slice_in_dim(attended, 0, local_rows * lax.axis_size("mp"), axis=0),
            out_weight,
            preferred_element_type=jnp.float32,
        ).astype(jnp.bfloat16),
        "mp",
        scatter_dimension=0,
        tiled=True,
    ).astype(jnp.float32)
    hidden, normed_one, inv_one = norm_forward(
        tokens.astype(jnp.float32) + branch_one + out_bias, first_gain, first_shift
    )
    hidden_low = hidden.astype(jnp.bfloat16)
    hidden_all = lax.all_gather(hidden_low, "mp", axis=0, tiled=True)
    pre_act = jnp.dot(hidden_all, up_weight, preferred_element_type=jnp.float32) + up_bias
    act_low = jax.nn.gelu(pre_act, approximate=False).astype(jnp.bfloat16)
    branch_two = lax.psum_scatter(
        jnp.dot(
            lax.slice_in_dim(act_low, 0, local_rows * lax.axis_size("mp"), axis=0),
            down_weight,
            preferred_element_type=jnp.float32,
        ).astype(jnp.bfloat16),
        "mp",
        scatter_dimension=0,
        tiled=True,
    ).astype(jnp.float32)
    layer_out, normed_two, inv_two = norm_forward(
        hidden + branch_two + down_bias, second_gain, second_shift
    )
    resid_two_grad, second_gain_grad, second_shift_grad = norm_backward(
        output_grad.astype(jnp.float32), normed_two, inv_two, second_gain
    )
    down_bias_grad = jnp.sum(resid_two_grad, 0)
    branch_two_low = resid_two_grad.astype(jnp.bfloat16)
    row_piece = lax.all_gather(branch_two_low, "mp", axis=0, tiled=True)
    row_start = jnp.int32(0)
    weight_acc = jnp.zeros(down_weight.shape, jnp.float32)
    act_acc = jnp.zeros(act_low.shape, jnp.float32)
    act_rows = lax.dynamic_slice_in_dim(act_low, row_start, row_piece.shape[0], 0)
    weight_acc = weight_acc + contract_rows(act_rows, row_piece)
    act_acc = lax.dynamic_update_slice_in_dim(
        act_acc, contract_cols(row_piece, down_weight), row_start, 0
    )
    down_weight_grad = weight_acc
    unused_two, gelu_back = jax.vjp(partial(jax.nn.gelu, approximate=False), pre_act)
    pre_grad = gelu_back(act_acc)[0].astype(jnp.bfloat16)
    up_bias_grad = jnp.sum(pre_grad, 0, dtype=jnp.float32)
    up_weight_grad = contract_rows(hidden_all, pre_grad)
    hidden_back = lax.psum_scatter(
        contract_cols(
            lax.slice_in_dim(pre_grad, 0, local_rows * lax.axis_size("mp"), axis=0), up_weight
        ).astype(jnp.bfloat16),
        "mp",
        scatter_dimension=0,
        tiled=True,
    ).astype(jnp.float32)
    hidden_grad = resid_two_grad + hidden_back
    resid_one_grad, first_gain_grad, first_shift_grad = norm_backward(
        hidden_grad, normed_one, inv_one, first_gain
    )
    out_bias_grad = jnp.sum(resid_one_grad, 0)
    branch_one_low = resid_one_grad.astype(jnp.bfloat16)
    row_piece = lax.all_gather(branch_one_low, "mp", axis=0, tiled=True)
    row_start = jnp.int32(0)
    weight_acc = jnp.zeros(out_weight.shape, jnp.float32)
    attn_acc = jnp.zeros(attended.shape, jnp.float32)
    attn_rows = lax.dynamic_slice_in_dim(attended, row_start, row_piece.shape[0], 0)
    weight_acc = weight_acc + contract_rows(attn_rows, row_piece)
    attn_acc = lax.dynamic_update_slice_in_dim(
        attn_acc, contract_cols(row_piece, out_weight), row_start, 0
    )
    out_weight_grad = weight_acc
    attn_low = attn_acc.astype(jnp.bfloat16)
    attn_low = attn_low.reshape(shape4)
    unused_three, (query_grad, key_grad, value_grad) = lax.scan(
        sequence_backward, 0, (queries, key_rows, values, attn_low, log_sums, lengths[0])
    )
    query_flat = query_grad.reshape(all_rows, head_cols)
    key_flat = key_grad.reshape(all_rows, head_cols)
    value_flat = value_grad.reshape(all_rows, head_cols)
    width_now = query_flat.shape[1]
    joint_grad = jnp.concatenate([query_flat, key_flat, value_flat], 1)
    query_bias_grad = jnp.sum(query_flat, 0, dtype=jnp.float32)
    value_bias_grad = jnp.sum(value_flat, 0, dtype=jnp.float32)
    joint_weight_grad = contract_rows(gathered, joint_grad)
    input_back = lax.psum_scatter(
        contract_cols(
            lax.slice_in_dim(joint_grad, 0, local_rows * lax.axis_size("mp"), axis=0), joint_weight
        ).astype(jnp.bfloat16),
        "mp",
        scatter_dimension=0,
        tiled=True,
    ).astype(jnp.float32)
    tokens_grad = (resid_one_grad + input_back).astype(jnp.bfloat16)
    query_weight_grad = joint_weight_grad[:, :width_now]
    key_weight_grad = joint_weight_grad[:, width_now : 2 * width_now]
    value_weight_grad = joint_weight_grad[:, 2 * width_now :]
    (
        query_weight_grad,
        query_bias_grad,
        key_weight_grad,
        value_weight_grad,
        value_bias_grad,
        out_weight_grad,
        up_weight_grad,
        up_bias_grad,
        down_weight_grad,
    ) = (
        lax.psum(query_weight_grad.astype(jnp.bfloat16), "dp").astype(jnp.float32),
        lax.psum(query_bias_grad.astype(jnp.bfloat16), "dp").astype(jnp.float32),
        lax.psum(key_weight_grad.astype(jnp.bfloat16), "dp").astype(jnp.float32),
        lax.psum(value_weight_grad.astype(jnp.bfloat16), "dp").astype(jnp.float32),
        lax.psum(value_bias_grad.astype(jnp.bfloat16), "dp").astype(jnp.float32),
        lax.psum(out_weight_grad.astype(jnp.bfloat16), "dp").astype(jnp.float32),
        lax.psum(up_weight_grad.astype(jnp.bfloat16), "dp").astype(jnp.float32),
        lax.psum(up_bias_grad.astype(jnp.bfloat16), "dp").astype(jnp.float32),
        lax.psum(down_weight_grad.astype(jnp.bfloat16), "dp").astype(jnp.float32),
    )
    (
        out_bias_grad,
        first_gain_grad,
        first_shift_grad,
        down_bias_grad,
        second_gain_grad,
        second_shift_grad,
    ) = lax.psum(
        (
            out_bias_grad,
            first_gain_grad,
            first_shift_grad,
            down_bias_grad,
            second_gain_grad,
            second_shift_grad,
        ),
        ("dp", "mp"),
    )
    return (
        layer_out.astype(jnp.bfloat16),
        tokens_grad,
        query_weight_grad,
        query_bias_grad,
        key_weight_grad,
        value_weight_grad,
        value_bias_grad,
        out_weight_grad,
        out_bias_grad,
        first_gain_grad,
        first_shift_grad,
        up_weight_grad,
        up_bias_grad,
        down_weight_grad,
        down_bias_grad,
        second_gain_grad,
        second_shift_grad,
    )


def solution(mesh):
    placed = (
        P(("dp", "mp"), None),
        P("dp", None),
        P(None, "mp"),
        P("mp"),
        P(None, "mp"),
        P(None, "mp"),
        P("mp"),
        P("mp", None),
        P(),
        P(),
        P(),
        P(None, "mp"),
        P("mp"),
        P("mp", None),
        P(),
        P(),
        P(),
        P(("dp", "mp"), None),
    )
    return jax.shard_map(
        per_device,
        mesh=mesh,
        in_specs=placed,
        out_specs=(
            P(("dp", "mp"), None),
            P(("dp", "mp"), None),
            P(None, "mp"),
            P("mp"),
            P(None, "mp"),
            P(None, "mp"),
            P("mp"),
            P("mp", None),
            P(),
            P(),
            P(),
            P(None, "mp"),
            P("mp"),
            P("mp", None),
            P(),
            P(),
            P(),
        ),
        check_vma=False,
    )
```

profile of v0, /device:TPU:0, one launch (start us, length us, event | category | flops | bytes accessed | tf_op | source)
XLA Modules:
  0.0 932.1 jit_solution(17560116255171023972)
XLA Ops:
  15.7 31.1 %all-gather.5.cloned.1.call-done = bf16[2048,1024]{1,0:T(8,128)(2,1)} async-done(((bf16[512,1024]{1,0:T(8,128)(2,1)}), bf16[2048,1024]{1,0:T(8,128)(2,1)}) %all-gather.5.cloned.1.call-update) | async-done | bytes 4194320 | tf_op jit(solution)/shard_map/all_gather | solution.py:145
  53.1 8.1 fusion.109
  61.2 8.1 fusion.110
  69.3 8.1 fusion.108
  77.5 23.7 %fusion.30 = (f32[4,512]{1,0:T(4,128)S(1)}, f32[4,512]{1,0:T(4,128)S(1)}, f32[4,512]{1,0:T(4,128)S(1)}, f32[4,512]{1,0:T(4,128)S(1)}, f32[4,512,2048]{2,1,0:T(8,128)}) fusion(pred[2048]{0:T(1024)(128)(4,1)S(1)} %iota_compare_fusion, f32[4,512,2048]{2,1,0:T(8,128)} %fusion.108, f32[4,512,2048]{2,1,0:T(8,128)} %fusion.109, f32[4,512,2048]{2,1,0:T(8,128)} %fusion.110, ...), kind=kOutput, calls=%fused_computation.61 | convolution fusion | flops 587194368 | bytes 68454400 | tf_op jit(solution)/shard_map/while/body/eval_jaxpr/qhd,khd->hqk/dot_general | solution.py:32
  101.2 24.7 %fusion = (f32[4,512]{1,0:T(4,128)S(1)}, f32[4,512]{1,0:T(4,128)S(1)}, f32[4,512]{1,0:T(4,128)S(1)}, f32[4,512]{1,0:T(4,128)S(1)}) fusion(f32[4,512]{1,0:T(4,128)S(1)} %get-tuple-element.102, f32[4,512,2048]{2,1,0:T(8,128)} %get-tuple-element.149, pred[2048]{0:T(1024)(128)(4,1)S(1)} %iota_compare_fusion, f32[4,512]{1,0:T(4,128)S(1)} %get-tuple-element.105, ...), kind=kLoop, calls=%fused_computation.24 | loop fusion | flops 67100672 | bytes 67176448 | tf_op jit(solution)/shard_map/while/body/eval_jaxpr/reduce_sum | solution.py:49
  126.0 8.1 fusion.70
  139.1 7.9 fusion.68
  147.0 8.0 fusion.69
  160.0 44.2 %reduce-scatter.5.cloned.1.call-done = bf16[512,1024]{1,0:T(8,128)(2,1)} async-done(((bf16[2048,1024]{1,0:T(8,128)(2,1)}), bf16[512,1024]{1,0:T(8,128)(2,1)}) %reduce-scatter.5.cloned.1.call-update) | async-done | bytes 1048592 | tf_op jit(solution)/shard_map/reduce_scatter | solution.py:156
  210.5 34.5 %all-gather.7.cloned.1.call-done = bf16[2048,1024]{1,0:T(8,128)(2,1)} async-done(((bf16[512,1024]{1,0:T(8,128)(2,1)}), bf16[2048,1024]{1,0:T(8,128)(2,1)}) %all-gather.7.cloned.1.call-update) | async-done | bytes 4194320 | tf_op jit(solution)/shard_map/all_gather | solution.py:170
  245.1 25.4 %multiply_convert_fusion.4 = (bf16[2048,1024]{1,0:T(8,128)(2,1)S(1)}, f32[2048,1024]{1,0:T(8,128)}, f32[2048,1024]{1,0:T(8,128)}) fusion(f32[1024]{0:T(1024)S(1)} %convert_element_type.240, bf16[2048,1024]{1,0:T(8,128)(2,1)} %all-gather.7.cloned.1.call-done, bf16[1024,1024]{1,0:T(8,128)(2,1)S(1)} %copy-done), kind=kOutput, calls=%fused_computation.43 | convolution fusion | flops 4433379328 | bytes 27267072 | tf_op jit(solution)/shard_map/dot_general | solution.py:171
  278.7 44.6 %reduce-scatter.7.cloned.1.call-done = bf16[512,1024]{1,0:T(8,128)(2,1)} async-done(((bf16[2048,1024]{1,0:T(8,128)(2,1)}), bf16[512,1024]{1,0:T(8,128)(2,1)}) %reduce-scatter.7.cloned.1.call-update) | async-done | bytes 1048592 | tf_op jit(solution)/shard_map/reduce_scatter | solution.py:173
  332.2 34.4 %all-gather.9.cloned.1.call-done = bf16[2048,1024]{1,0:T(8,128)(2,1)} async-done(((bf16[512,1024]{1,0:T(8,128)(2,1)}), bf16[2048,1024]{1,0:T(8,128)(2,1)}) %all-gather.9.cloned.1.call-update) | async-done | bytes 4194320 | tf_op jit(solution)/shard_map/all_gather | solution.py:191
  366.6 13.9 %fusion.96 = (bf16[1024]{0:T(1024)(128)(2,1)}, bf16[2048,1024]{1,0:T(8,128)(2,1)S(1)}) fusion(f32[2048,1024]{1,0:T(8,128)} %get-tuple-element.130, f32[2048,1024]{1,0:T(8,128)} %get-tuple-element.150, f32[1024]{0:T(1024)S(1)} %convert_element_type.240, bf16[2048,1024]{1,0:T(8,128)(2,1)} %all-gather.9.cloned.1.call-done, bf16[1024,1024]{1,0:T(8,128)(2,1)} %param.31), kind=kOutput, calls=%fused_computation.177 | convolution fusion | flops 4328520704 | bytes 27269120 | tf_op jit(solution)/shard_map/dot_general | solution.py:106
  388.8 44.7 %reduce-scatter.9.cloned.1.call-done = bf16[512,1024]{1,0:T(8,128)(2,1)} async-done(((bf16[2048,1024]{1,0:T(8,128)(2,1)}), bf16[512,1024]{1,0:T(8,128)(2,1)}) %reduce-scatter.9.cloned.1.call-update) | async-done | bytes 1048592 | tf_op jit(solution)/shard_map/reduce_scatter | solution.py:205
  443.8 9.6 %convolution_convert_fusion.5 = bf16[1024,1024]{1,0:T(8,128)(2,1)} fusion(bf16[2048,1024]{1,0:T(8,128)(2,1)} %copy-done.52, bf16[2048,1024]{1,0:T(8,128)(2,1)} %all-gather.9.cloned.1.call-done), kind=kOutput, calls=%fused_computation.109 | convolution fusion | flops 4296015872 | bytes 10485760 | tf_op jit(solution)/shard_map/dot_general | solution.py:100
  459.5 18.7 %all-gather.11.cloned.1.call-done = bf16[2048,1024]{1,0:T(8,128)(2,1)} async-done(((bf16[512,1024]{1,0:T(8,128)(2,1)}), bf16[2048,1024]{1,0:T(8,128)(2,1)}) %all-gather.11.cloned.1.call-update) | async-done | bytes 4194320 | tf_op jit(solution)/shard_map/all_gather | solution.py:219
  481.8 8.2 fusion.112
  490.0 9.0 fusion.13
  499.0 8.2 fusion.113
  507.2 8.1 fusion.111
  515.3 38.5 %multiply_reduce_fusion = (f32[4,512]{1,0:T(4,128)S(1)}, f32[4,512]{1,0:T(4,128)S(1)}, f32[4,512]{1,0:T(4,128)S(1)}, f32[4,512]{1,0:T(4,128)S(1)}, f32[4,512,2048]{2,1,0:T(8,128)}) fusion(f32[4,512]{1,0:T(4,128)S(1)} %get-tuple-element.162, f32[4,512,2048]{2,1,0:T(8,128)S(1)} %bitcast.106, pred[2048]{0:T(1024)(128)(4,1)S(1)} %iota_compare_fusion, ...), kind=kOutput, calls=%fused_computation.1 | convolution fusion | flops 620748800 | bytes 135596032 | tf_op jit(solution)/shard_map/while/body/eval_jaxpr/qhd,khd->hqk/dot_general | solution.py:74
  553.8 51.7 %multiply_convert_fusion = (bf16[4,512,2048]{2,1,0:T(8,128)(2,1)}, bf16[4,512,2048]{2,1,0:T(8,128)(2,1)}, bf16[4,512,2048]{2,1,0:T(8,128)(2,1)}, bf16[4,512,2048]{2,1,0:T(8,128)(2,1)S(1)}) fusion(f32[4,512,2048]{2,1,0:T(8,128)} %get-tuple-element.151, f32[4,512]{1,0:T(4,128)S(1)} %get-tuple-element.94, f32[4,512]{1,0:T(4,128)S(1)} %get-tuple-element.162, ...), kind=kLoop, calls=%fused_computation | loop fusion | flops 100663296 | bytes 167839744 | tf_op jit(solution)/shard_map/while/body/eval_jaxpr/convert_element_type | solution.py:75
  611.3 9.4 %fusion.38 = f32[4,64,2048]{2,1,0:T(8,128)} fusion(f32[4,64,2048]{2,1,0:T(8,128)S(1)} %copy-done.51, bf16[512,4,64]{0,2,1:T(8,128)(2,1)S(1)} %bitcast.146, f32[4,512]{1,0:T(4,128)S(1)} %get-tuple-element.165, f32[4,512,2048]{2,1,0:T(8,128)} %get-tuple-element.149, pred[2048]{0:T(1024)(128)(4,1)S(1)} %iota_compare_fusion), kind=kOutput, calls=%fused_computation.81 | convolution fusion | flops 554172416 | bytes 21243904 | tf_op jit(solution)/shard_map/while/body/eval_jaxpr/hqk,qhd->khd/dot_general | solution.py:71
  620.8 8.8 fusion.41
  634.0 6.5 fusion.104
  663.7 7.2 convolution_convert_fusion.1
  671.0 43.9 %all-reduce = (f32[1024]{0:T(1024)}, f32[1024]{0:T(1024)}, f32[1024]{0:T(1024)}, f32[1024]{0:T(1024)}, f32[1024]{0:T(1024)}, /*index=5*/f32[1024]{0:T(1024)}) all-reduce(f32[1024]{0:T(1024)S(1)} %copy-done.34, f32[1024]{0:T(1024)S(1)} %copy-done.35, f32[1024]{0:T(1024)S(1)} %copy-done.36, ...), channel_id=1, replica_groups=mesh['dp'=8,'mp'=4] {'dp','mp'}, use_global_device_ids=true, to_apply=%region_36.37 | all-reduce | flops 6144 | bytes 49152 | tf_op jit(solution)/shard_map/psum | solution.py:282
  715.0 21.7 %all-reduce.1 = (bf16[256]{0:T(256)(128)(2,1)S(1)}, bf16[256]{0:T(256)(128)(2,1)S(1)}, bf16[1024]{0:T(1024)(128)(2,1)S(1)}) all-reduce(bf16[256]{0:T(256)(128)(2,1)S(1)} %reduce_sum.299, bf16[256]{0:T(256)(128)(2,1)S(1)} %reduce_sum.301, bf16[1024]{0:T(1024)(128)(2,1)S(1)} %copy-done.45), channel_id=1, replica_groups=mesh['dp'=8,'mp'=4] {'dp'}, use_global_device_ids=true, to_apply=%region_29.30 | all-reduce | flops 1536 | bytes 6144 | tf_op jit(solution)/shard_map/psum | solution.py:266
  738.5 137.3 %all-reduce.5.cloned.1.call-done = (bf16[1024,256]{0,1:T(8,128)(2,1)}, bf16[1024,256]{0,1:T(8,128)(2,1)}, bf16[1024,256]{0,1:T(8,128)(2,1)}, bf16[256,1024]{1,0:...) async-done(((bf16[1024,256]{0,1:T(8,128)(2,1)}, bf16[1024,256]{0,1:T(8,128)(2,1)}, bf16[1024,256]{0,1:T(8,128)(2,1)}, bf16[256,1024]{1,0:T(8,128)(2,1)}, ...) | async-done | bytes 6291472 | tf_op jit(solution)/shard_map/psum | solution.py:265
  892.1 29.8 %reduce-scatter.11.cloned.1.call-done = bf16[512,1024]{1,0:T(8,128)(2,1)} async-done(((bf16[2048,1024]{1,0:T(8,128)(2,1)}), bf16[512,1024]{1,0:T(8,128)(2,1)}) %reduce-scatter.11.cloned.1.call-update) | async-done | bytes 1048592 | tf_op jit(solution)/shard_map/reduce_scatter | solution.py:242
  (239 shorter events, 130.0 us)
Async XLA Ops:
  7.2 237.9 %copy-start = (bf16[1024,1024]{1,0:T(8,128)(2,1)S(1)}, bf16[1024,1024]{1,0:T(8,128)(2,1)}, u32[]{:S(2)}) copy-start(bf16[1024,1024]{1,0:T(8,128)(2,1)} %param.29) | copy-start | bytes 6291460
  7.2 39.6 %all-gather.5.cloned.1.call-start = ((), (), s32[]{:S(2)}) async-start(), calls=%async_computation.4 | async-start | bytes 5242880 | tf_op jit(solution)/shard_map/all_gather | solution.py:145
  7.9 196.3 %reduce-scatter.5.cloned.1.call-start = ((), (), s32[]{:S(2)}) async-start(), calls=%async_computation.5 | async-start | bytes 5242880 | tf_op jit(solution)/shard_map/reduce_scatter | solution.py:156
  52.7 24.8 %copy-start.2 = (bf16[2048,256]{0,1:T(8,128)(2,1)}, bf16[2048,256]{0,1:T(8,128)(2,1)S(1)}, u32[]{:S(2)}) copy-start(bf16[2048,256]{0,1:T(8,128)(2,1)S(1)} %slice.137) | copy-start | bytes 3145732
  53.0 94.0 %copy-start.6 = (bf16[2048,256]{0,1:T(8,128)(2,1)}, bf16[2048,256]{0,1:T(8,128)(2,1)S(1)}, u32[]{:S(2)}) copy-start(bf16[2048,256]{0,1:T(8,128)(2,1)S(1)} %get-tuple-element.132) | copy-start | bytes 3145732
  53.1 16.2 %copy-start.17 = (bf16[512,256]{0,1:T(8,128)(2,1)}, bf16[512,256]{0,1:T(8,128)(2,1)S(1)}, u32[]{:S(2)}) copy-start(bf16[512,256]{0,1:T(8,128)(2,1)S(1)} %get-tuple-element.143) | copy-start | bytes 786436
  53.1 24.3 %copy-start.19 = (bf16[512,256]{0,1:T(8,128)(2,1)}, bf16[512,256]{0,1:T(8,128)(2,1)S(1)}, u32[]{:S(2)}) copy-start(bf16[512,256]{0,1:T(8,128)(2,1)S(1)} %get-tuple-element.144) | copy-start | bytes 786436
  101.2 24.8 %copy-start.24 = (f32[4,512]{1,0:T(4,128)}, f32[4,512]{1,0:T(4,128)S(1)}, u32[]{:S(2)}) copy-start(f32[4,512]{1,0:T(4,128)S(1)} %get-tuple-element.104) | copy-start | bytes 24580
  101.2 32.9 %copy-start.26 = (f32[4,512]{1,0:T(4,128)}, f32[4,512]{1,0:T(4,128)S(1)}, u32[]{:S(2)}) copy-start(f32[4,512]{1,0:T(4,128)S(1)} %get-tuple-element.105) | copy-start | bytes 24580
  101.2 32.9 %slice-start = ((s8[16777216]{0:T(1024)(128)(4,1)}), s8[4194304]{0:T(1024)(128)(4,1)S(1)}, s32[]{:S(2)}) async-start(s8[16777216]{0:T(1024)(128)(4,1)} %bitcast.103), calls=%async_computation.13 | async-start | bytes 8388608
  101.2 32.9 %slice-start.1 = ((s8[16777216]{0:T(1024)(128)(4,1)}), s8[4194304]{0:T(1024)(128)(4,1)S(1)}, s32[]{:S(2)}) async-start(s8[16777216]{0:T(1024)(128)(4,1)} %bitcast.103), calls=%async_computation.14 | async-start | bytes 8388608
  155.0 49.2 %copy-start.4 = (bf16[512,1024]{1,0:T(8,128)(2,1)S(1)}, bf16[512,1024]{1,0:T(8,128)(2,1)}, u32[]{:S(2)}) copy-start(bf16[512,1024]{1,0:T(8,128)(2,1)} %param.18) | copy-start | bytes 3145732
  159.5 51.1 %copy-start.41 = (bf16[1024]{0:T(1024)(128)(2,1)S(1)}, bf16[1024]{0:T(1024)(128)(2,1)}, u32[]{:S(2)}) copy-start(bf16[1024]{0:T(1024)(128)(2,1)} %param.30) | copy-start | bytes 6148
  159.5 85.6 %all-gather.7.cloned.1.call-start = ((), (), s32[]{:S(2)}) async-start(), calls=%async_computation.6 | async-start | bytes 5242880 | tf_op jit(solution)/shard_map/all_gather | solution.py:170
  210.5 112.8 %reduce-scatter.7.cloned.1.call-start = ((), (), s32[]{:S(2)}) async-start(), calls=%async_computation.7 | async-start | bytes 5242880 | tf_op jit(solution)/shard_map/reduce_scatter | solution.py:173
  245.1 27.4 %copy-start.49 = (bf16[1024,1024]{1,0:T(8,128)(2,1)S(1)}, bf16[1024,1024]{1,0:T(8,128)(2,1)}, u32[]{:S(2)}) copy-start(bf16[1024,1024]{1,0:T(8,128)(2,1)} %param.31) | copy-start | bytes 6291460
  278.6 88.0 %all-gather.9.cloned.1.call-start = ((), (), s32[]{:S(2)}) async-start(), calls=%async_computation.8 | async-start | bytes 5242880 | tf_op jit(solution)/shard_map/all_gather | solution.py:191
  332.0 101.5 %reduce-scatter.9.cloned.1.call-start = ((), (), s32[]{:S(2)}) async-start(), calls=%async_computation.9 | async-start | bytes 5242880 | tf_op jit(solution)/shard_map/reduce_scatter | solution.py:205
  388.7 49.0 %copy-start.5 = (bf16[512,1024]{1,0:T(8,128)(2,1)S(1)}, bf16[512,1024]{1,0:T(8,128)(2,1)}, u32[]{:S(2)}) copy-start(bf16[512,1024]{1,0:T(8,128)(2,1)} %reduce-scatter.5.cloned.1.call-done) | copy-start | bytes 3145732
  388.8 89.5 %all-gather.11.cloned.1.call-start = ((), (), s32[]{:S(2)}) async-start(), calls=%async_computation.10 | async-start | bytes 5242880 | tf_op jit(solution)/shard_map/all_gather | solution.py:219
  443.6 432.2 %all-reduce.5.cloned.1.call-start = ((), (), s32[]{:S(2)}) async-start(), calls=%async_computation.12 | async-start | bytes 12582912 | tf_op jit(solution)/shard_map/psum | solution.py:265
  453.3 24.9 %copy-start.23 = (bf16[256,1024]{1,0:T(8,128)(2,1)S(1)}, bf16[256,1024]{1,0:T(8,128)(2,1)}, u32[]{:S(2)}) copy-start(bf16[256,1024]{1,0:T(8,128)(2,1)} %param.25) | copy-start | bytes 1572868
  459.5 22.3 %copy-start.7 = (bf16[2048,256]{0,1:T(8,128)(2,1)S(1)}, bf16[2048,256]{0,1:T(8,128)(2,1)}, u32[]{:S(2)}) copy-start(bf16[2048,256]{0,1:T(8,128)(2,1)} %copy-done.6) | copy-start | bytes 3145732
  499.0 16.3 %slice-start.4 = ((s8[16777216]{0:T(1024)(128)(4,1)}), s8[4194304]{0:T(1024)(128)(4,1)S(1)}, s32[]{:S(2)}) async-start(s8[16777216]{0:T(1024)(128)(4,1)} %bitcast.105), calls=%async_computation.17 | async-start | bytes 8388608
  499.0 16.3 %slice-start.5 = ((s8[16777216]{0:T(1024)(128)(4,1)}), s8[4194304]{0:T(1024)(128)(4,1)S(1)}, s32[]{:S(2)}) async-start(s8[16777216]{0:T(1024)(128)(4,1)} %bitcast.105), calls=%async_computation.18 | async-start | bytes 8388608
  553.8 51.7 %copy-start.3 = (bf16[2048,256]{0,1:T(8,128)(2,1)S(1)}, bf16[2048,256]{0,1:T(8,128)(2,1)}, u32[]{:S(2)}) copy-start(bf16[2048,256]{0,1:T(8,128)(2,1)} %copy-done.2) | copy-start | bytes 3145732
  611.3 18.2 %slice-start.8 = ((s8[16777216]{0:T(1024)(128)(4,1)}), s8[4194304]{0:T(1024)(128)(4,1)S(1)}, s32[]{:S(2)}) async-start(s8[16777216]{0:T(1024)(128)(4,1)} %bitcast.107), calls=%async_computation.21 | async-start | bytes 8388608
  611.3 18.2 %slice-start.9 = ((s8[16777216]{0:T(1024)(128)(4,1)}), s8[4194304]{0:T(1024)(128)(4,1)S(1)}, s32[]{:S(2)}) async-start(s8[16777216]{0:T(1024)(128)(4,1)} %bitcast.107), calls=%async_computation.22 | async-start | bytes 8388608
  633.9 22.3 %copy-start.50 = (bf16[4,64,2048]{2,1,0:T(8,128)(2,1)}, bf16[4,64,2048]{2,1,0:T(8,128)(2,1)S(1)}, u32[]{:S(2)}) copy-start(bf16[4,64,2048]{2,1,0:T(8,128)(2,1)S(1)} %get-tuple-element.161) | copy-start | bytes 3145732
  663.6 51.4 %copy-start.45 = (bf16[1024]{0:T(1024)(128)(2,1)S(1)}, bf16[1024]{0:T(1024)(128)(2,1)}, u32[]{:S(2)}) copy-start(bf16[1024]{0:T(1024)(128)(2,1)} %get-tuple-element.123) | copy-start | bytes 6148
  663.7 258.3 %reduce-scatter.11.cloned.1.call-start = ((), (), s32[]{:S(2)}) async-start(), calls=%async_computation.11 | async-start | bytes 5242880 | tf_op jit(solution)/shard_map/reduce_scatter | solution.py:242
  884.8 40.3 %copy-start.1 = (bf16[1024,1024]{1,0:T(8,128)(2,1)S(1)}, bf16[1024,1024]{1,0:T(8,128)(2,1)}, u32[]{:S(2)}) copy-start(bf16[1024,1024]{1,0:T(8,128)(2,1)} %param.29) | copy-start | bytes 6291460
  (50 other events, 323.8 us)
Sparse Core Ops, SparseCore 0:
  9.6 37.1 all-gather.4
  159.6 44.5 reduce-scatter.4
  210.6 34.4 all-gather.6
  278.7 44.5 reduce-scatter.6
  332.1 34.4 all-gather.8
  388.9 44.5 reduce-scatter.8
  443.7 34.4 all-gather.10
  663.7 212.0 all-reduce.4
  878.4 43.5 reduce-scatter.10
where the time goes:
time: 941 us; the launch traced here: 932 us
  waiting for transfers between devices  420 us (45%)
  matrix products  290 us (31%)
  other arithmetic  117 us (12%)
  blocking collectives  65.6 us (7%)
  local copies, waits for them, and re-layouts  23 us (2%)
  between operations  15.9 us (2%)
    psum x1, waiting for transfers between devices, per_device(): lax.psum(query_weight_grad.astype(jnp.bfloat16), 'dp').astype(jnp.float32)  137 us
    dot_general x4, matrix products, sequence_backward(): jnp.einsum('qhd,khd->hqk', grad_blk, values, preferred_element_type=jnp.f...  63 us
    convert_element_type x1, other arithmetic, sequence_backward(): (probs * (prob_grad - jnp.sum(probs * prob_grad, -1, keepdims=True))).ast...  51.7 us
    dot_general x4, matrix products, masked_scores(): jnp.einsum('qhd,khd->hqk', query_blk, key_rows, preferred_element_type=jn...  48 us
    reduce_scatter x1, waiting for transfers between devices, per_device(): lax.psum_scatter(contract_cols(lax.slice_in_dim(pre_grad, 0, local_rows *...  44.7 us
    reduce_scatter x1, waiting for transfers between devices, per_device(): lax.psum_scatter(jnp.dot(lax.slice_in_dim(act_low, 0, local_rows * lax.ax...  44.6 us
    reduce_scatter x1, waiting for transfers between devices, per_device(): lax.psum_scatter(jnp.dot(lax.slice_in_dim(attended, 0, local_rows * lax.a...  44.2 us
    psum x1, blocking collectives, per_device(): lax.psum((out_bias_grad, first_gain_grad, first_shift_grad, down_bias_gra...  43.9 us
  transfers between devices with their start and end apart: 9, of which 9 were waited for; matrix products, arithmetic and copies ran while one was open for 5% of the time, Pallas kernels for 0%

commit v1 on v0

--- a/solution.py
+++ b/solution.py
@@ -3,6 +3,8 @@
 import jax
 import jax.numpy as jnp
 from jax import lax
+from jax.experimental import pallas as pl
+from jax.experimental.pallas import tpu as pltpu
 from jax.sharding import PartitionSpec as P
 
 HD = 64
@@ -28,72 +30,186 @@
     return (back, jnp.sum(grad * normed, 0), jnp.sum(grad, 0))
 
 
-def masked_scores(query_blk, key_rows, length):
-    scores = jnp.einsum(
-        "qhd,khd->hqk", query_blk, key_rows, preferred_element_type=jnp.float32
-    ) * HD ** (-0.5)
-    valid = lax.iota(jnp.int32, key_rows.shape[0]) < length
-    return jnp.where(valid[None, None, :], scores, -1000000000.0)
-
-
-def sequence_forward(carried, inputs):
-    queries, key_rows, values, length = inputs
-    seq_len = queries.shape[0]
-    block_rows = min(512, seq_len)
-    outputs = []
-    log_sums = []
-    for offset in range(0, seq_len, block_rows):
-        scores = masked_scores(queries[offset : offset + block_rows], key_rows, length)
-        row_max = jnp.max(scores, -1, keepdims=True)
-        expon = jnp.exp(scores - row_max)
-        row_sum = jnp.sum(expon, -1, keepdims=True)
-        probs = (expon / row_sum).astype(jnp.bfloat16)
-        outputs.append(
-            jnp.einsum("hqk,khd->qhd", probs, values, preferred_element_type=jnp.float32)
-        )
-        log_sums.append((row_max + jnp.log(row_sum))[..., 0])
-    return (carried, (jnp.concatenate(outputs, 0), jnp.concatenate(log_sums, 1)))
-
-
-def sequence_backward(carried, inputs):
-    queries, key_rows, values, out_grad, log_sums, length = inputs
-    seq_len = queries.shape[0]
-    block_rows = min(512, seq_len)
-    scale = HD ** (-0.5)
-    key_grad = jnp.zeros(key_rows.shape, jnp.float32)
-    value_grad = jnp.zeros(values.shape, jnp.float32)
+F32 = jnp.float32
+BF = jnp.bfloat16
+MASKED = -1000000000.0
+WIDE = 2 * HD
+
+
+def mm(a, b, ca, cb):
+    return lax.dot_general(a, b, (((ca,), (cb,)), ((), ())), preferred_element_type=F32)
+
+
+def forward_kernel(heads, len_ref, q_ref, k_ref, vt_ref, e_ref, o_ref, r_ref, v_aug, k_aug):
+    seq, step = pl.program_id(0), pl.program_id(2)
+    seq_len, block = k_ref.shape[0], q_ref.shape[0]
+
+    @pl.when(step == 0)
+    def _():
+        rows = lax.broadcasted_iota(jnp.int32, (seq_len, WIDE), 0)
+        lanes = lax.broadcasted_iota(jnp.int32, (seq_len, WIDE), 1)
+        bias = jnp.where(rows < len_ref[seq], 0.0, MASKED)
+        keys = k_ref[...].astype(F32)
+        for h in range(heads):
+            other = (1 - h) * HD
+            k_aug[h] = jnp.where(
+                lanes // HD == h, keys, jnp.where(lanes == other, bias, 0.0)
+            ).astype(BF)
+            v_aug[h, :HD] = vt_ref[h * HD : (h + 1) * HD, :]
+            v_aug[h, HD:] = jnp.ones((16, seq_len), BF)
+
+    query = q_ref[...].astype(F32) * HD**-0.5
+    lanes = lax.broadcasted_iota(jnp.int32, (block, WIDE), 1)
+    scores = []
+    for h in range(heads):
+        other = (1 - h) * HD
+        q_aug = jnp.where(
+            lanes // HD == h, query, jnp.where(lanes == other, 1.0, 0.0)
+        ).astype(BF)
+        scores.append(mm(k_aug[h], q_aug, 1, 1))
+    outs = []
+    for h in range(heads):
+        top = jnp.max(scores[h], 0, keepdims=True)
+        expon = jnp.exp(scores[h] - top).astype(BF)
+        e_ref[h] = expon
+        total = mm(v_aug[h], expon, 1, 0)
+        inverse = 1.0 / total[HD : HD + 1]
+        r_ref[h] = inverse
+        outs.append(total[:HD] * inverse)
+    if heads == 1:
+        outs.append(jnp.zeros_like(outs[0]))
+    o_ref[...] = jnp.concatenate(outs, 0).T.astype(BF)
+
+
+def backward_kernel(
+    heads, e_ref, r_ref, q_ref, k_ref, v_ref, o_ref, g_ref, dq_ref, dk_ref, dv_ref, v_aug, k_t, dks, dvs
+):
+    step, last = pl.program_id(2), pl.num_programs(2) - 1
+    seq_len, block = k_ref.shape[0], q_ref.shape[0]
+
+    @pl.when(step == 0)
+    def _():
+        lanes = lax.broadcasted_iota(jnp.int32, (seq_len, WIDE), 1)
+        values = v_ref[...].astype(F32)
+        for h in range(heads):
+            other = (1 - h) * HD
+            ones = jnp.where((lanes >= other) & (lanes < other + 2), 1.0, 0.0)
+            v_aug[h] = jnp.where(lanes // HD == h, values, ones).astype(BF)
+        k_t[...] = (k_ref[...].astype(F32) * HD**-0.5).T.astype(BF)
+        dks[...] = jnp.zeros_like(dks)
+        dvs[...] = jnp.zeros_like(dvs)
+
+    lanes = lax.broadcasted_iota(jnp.int32, (block, WIDE), 1)
+    inverse = jnp.concatenate(
+        [jnp.broadcast_to(r_ref[h % heads], (HD, block)) for h in range(2)], 0
+    ).T
+    grad = (g_ref[...].astype(F32) * inverse).astype(BF)
+    grad_wide = grad.astype(F32)
+    scaled_query = (q_ref[...].astype(F32) * HD**-0.5).astype(BF)
+    product = grad_wide * o_ref[...].astype(F32)
+    centered = []
+    for h in range(heads):
+        other = (1 - h) * HD
+        inside = lanes // HD == h
+        row_dot = jnp.sum(jnp.where(inside, product, 0.0), -1, keepdims=True)
+        high = row_dot.astype(BF).astype(F32)
+        g_aug = jnp.where(
+            inside,
+            grad_wide,
+            jnp.where(lanes == other, -high, jnp.where(lanes == other + 1, high - row_dot, 0.0)),
+        ).astype(BF)
+        centered.append(mm(v_aug[h], g_aug, 1, 1))
     query_grads = []
-    for offset in range(0, seq_len, block_rows):
-        query_blk = queries[offset : offset + block_rows]
-        grad_blk = out_grad[offset : offset + block_rows]
-        scores = masked_scores(query_blk, key_rows, length)
-        probs = jnp.exp(scores - log_sums[:, offset : offset + block_rows, None])
-        value_grad = value_grad + jnp.einsum(
-            "hqk,qhd->khd", probs.astype(jnp.bfloat16), grad_blk, preferred_element_type=jnp.float32
-        )
-        prob_grad = jnp.einsum("qhd,khd->hqk", grad_blk, values, preferred_element_type=jnp.float32)
-        score_grad = (probs * (prob_grad - jnp.sum(probs * prob_grad, -1, keepdims=True))).astype(
-            jnp.bfloat16
-        )
-        query_grads.append(
-            (
-                jnp.einsum("hqk,khd->qhd", score_grad, key_rows, preferred_element_type=jnp.float32)
-                * scale
-            ).astype(jnp.bfloat16)
-        )
-        key_grad = (
-            key_grad
-            + jnp.einsum("hqk,qhd->khd", score_grad, query_blk, preferred_element_type=jnp.float32)
-            * scale
-        )
-    return (
-        carried,
-        (
-            jnp.concatenate(query_grads, 0),
-            key_grad.astype(jnp.bfloat16),
-            value_grad.astype(jnp.bfloat16),
+    for h in range(heads):
+        cols = slice(h * HD, (h + 1) * HD)
+        expon = e_ref[h]
+        score_grad = (expon.astype(F32) * centered[h]).astype(BF)
+        dvs[h] += mm(expon, grad[:, cols], 1, 0)
+        dks[h] += mm(score_grad, scaled_query[:, cols], 1, 0)
+        query_grads.append(mm(k_t[cols, :], score_grad, 1, 0))
+    if heads == 1:
+        query_grads.append(jnp.zeros_like(query_grads[0]))
+    dq_ref[...] = jnp.concatenate(query_grads, 0).T.astype(BF)
+
+    @pl.when(step == last)
+    def _():
+        for total, out in ((dks, dk_ref), (dvs, dv_ref)):
+            halves = [total[h] for h in range(heads)]
+            if heads == 1:
+                halves.append(jnp.zeros_like(halves[0]))
+            out[...] = jnp.concatenate(halves, 1).astype(BF)
+
+
+def attention_shape(rows, cols, seqs):
+    seq_len = rows // seqs
+    block = min(512, seq_len)
+    steps = seq_len // block
+    pairs = max(1, cols // WIDE)
+    heads = cols // HD // pairs
+    row_spec = pl.BlockSpec((block, WIDE), lambda s, p, j, *_: (s * steps + j, p))
+    key_spec = pl.BlockSpec((seq_len, WIDE), lambda s, p, j, *_: (s, p))
+    e_spec = pl.BlockSpec((heads, seq_len, block), lambda s, p, j, *_: (p, s, j))
+    r_spec = pl.BlockSpec((heads, 1, block), lambda s, p, j, *_: (p, 0, s * steps + j))
+    return seq_len, heads, pairs, (seqs, pairs, steps), row_spec, key_spec, e_spec, r_spec
+
+
+def widen(array):
+    short = WIDE - array.shape[1]
+    return array if short <= 0 else jnp.pad(array, ((0, 0), (0, short)))
+
+
+def attention_forward(queries, keys, values, lengths):
+    rows, cols = queries.shape
+    seqs = lengths.shape[0]
+    seq_len, heads, pairs, grid, row_spec, key_spec, e_spec, r_spec = attention_shape(rows, cols, seqs)
+    wide_cols = pairs * WIDE
+    expon, attended, inverse = pl.pallas_call(
+        partial(forward_kernel, heads),
+        grid_spec=pltpu.PrefetchScalarGridSpec(
+            num_scalar_prefetch=1,
+            grid=grid,
+            in_specs=[
+                row_spec,
+                key_spec,
+                pl.BlockSpec((WIDE, seq_len), lambda s, p, j, *_: (p, s)),
+            ],
+            out_specs=[e_spec, row_spec, r_spec],
+            scratch_shapes=[
+                pltpu.VMEM((heads, HD + 16, seq_len), BF),
+                pltpu.VMEM((heads, seq_len, WIDE), BF),
+            ],
         ),
-    )
+        out_shape=[
+            jax.ShapeDtypeStruct((heads * pairs, rows, seq_len), BF),
+            jax.ShapeDtypeStruct((rows, wide_cols), BF),
+            jax.ShapeDtypeStruct((heads * pairs, 1, rows), F32),
+        ],
+        name="attention_forward",
+        compiler_params=pltpu.CompilerParams(vmem_limit_bytes=60 * 1024 * 1024),
+    )(lengths, widen(queries), widen(keys), widen(values).T)
+    return expon, attended[:, :cols], inverse
+
+
+def attention_backward(expon, inverse, queries, keys, values, attended, grad, seqs):
+    rows, cols = queries.shape
+    seq_len, heads, pairs, grid, row_spec, key_spec, e_spec, r_spec = attention_shape(rows, cols, seqs)
+    shape = jax.ShapeDtypeStruct((rows, pairs * WIDE), BF)
+    outs = pl.pallas_call(
+        partial(backward_kernel, heads),
+        grid=grid,
+        in_specs=[e_spec, r_spec, row_spec, key_spec, key_spec, row_spec, row_spec],
+        out_specs=[row_spec, key_spec, key_spec],
+        scratch_shapes=[
+            pltpu.VMEM((heads, seq_len, WIDE), BF),
+            pltpu.VMEM((WIDE, seq_len), BF),
+            pltpu.VMEM((heads, seq_len, HD), F32),
+            pltpu.VMEM((heads, seq_len, HD), F32),
+        ],
+        out_shape=[shape] * 3,
+        name="attention_backward",
+        compiler_params=pltpu.CompilerParams(vmem_limit_bytes=60 * 1024 * 1024),
+    )(expon, inverse, *[widen(x) for x in (queries, keys, values, attended, grad)])
+    return [x[:, :cols] for x in outs]
 
 
 def contract_rows(left, right):
@@ -137,22 +253,13 @@
 ):
     local_rows = tokens.shape[0]
     head_cols = query_weight.shape[1]
-    heads_here = head_cols // HD
     seq_count = lengths.shape[1]
     all_rows = local_rows * lax.axis_size("mp")
-    seq_len = all_rows // seq_count
-    shape4 = (seq_count, seq_len, heads_here, HD)
     gathered = lax.all_gather(tokens, "mp", axis=0, tiled=True)
     joint_weight = jnp.concatenate([query_weight, key_weight, value_weight], 1)
     projected = jnp.dot(gathered, joint_weight, preferred_element_type=jnp.float32)
     queries, key_rows, values = split_projection(projected, head_cols, query_bias, value_bias)
-    queries = queries.reshape(shape4)
-    key_rows = key_rows.reshape(shape4)
-    values = values.reshape(shape4)
-    unused_one, (attended, log_sums) = lax.scan(
-        sequence_forward, 0, (queries, key_rows, values, lengths[0])
-    )
-    attended = attended.reshape(all_rows, head_cols).astype(jnp.bfloat16)
+    expon, attended, inverse = attention_forward(queries, key_rows, values, lengths[0])
     branch_one = lax.psum_scatter(
         jnp.dot(
             lax.slice_in_dim(attended, 0, local_rows * lax.axis_size("mp"), axis=0),
@@ -227,13 +334,9 @@
     )
     out_weight_grad = weight_acc
     attn_low = attn_acc.astype(jnp.bfloat16)
-    attn_low = attn_low.reshape(shape4)
-    unused_three, (query_grad, key_grad, value_grad) = lax.scan(
-        sequence_backward, 0, (queries, key_rows, values, attn_low, log_sums, lengths[0])
-    )
-    query_flat = query_grad.reshape(all_rows, head_cols)
-    key_flat = key_grad.reshape(all_rows, head_cols)
-    value_flat = value_grad.reshape(all_rows, head_cols)
+    query_flat, key_flat, value_flat = attention_backward(
+        expon, inverse, queries, key_rows, values, attended, attn_low, seq_count
+    )
     width_now = query_flat.shape[1]
     joint_grad = jnp.concatenate([query_flat, key_flat, value_flat], 1)
     query_bias_grad = jnp.sum(query_flat, 0, dtype=jnp.float32)

time: 941 us -> 739 us (0.79)
  matrix products: 290 us -> 94.3 us
  other arithmetic: 117 us -> 35.3 us
  Pallas kernels: 0 us -> 75.5 us
    dot_general x24 -> x0, matrix products: 197 us -> none  [the longest x4 63 us: sequence_backward(): jnp.einsum('qhd,khd->hqk', grad_blk, values, preferred_element_type=jnp.f...]
    pallas_call x0 -> x2, Pallas kernels: none -> 75.5 us  [the longest x1 42.2 us: attention_backward(): pl.pallas_call(partial(backward_kernel, heads), grid=grid, in_specs=[e_sp...]
    convert_element_type x1 -> x0, other arithmetic: 51.7 us -> none  [sequence_backward(): (probs * (prob_grad - jnp.sum(probs * prob_grad, -1, keepdims=True))).ast...]
    reduce_sum x1, other arithmetic: 24.7 us -> 0.39 us  [per_device(): value_bias_grad = jnp.sum(value_flat, 0, dtype=jnp.float32)]
    unnamed x151 -> x64, local copies, waits for them, and re-layouts: 19.3 us -> 18.5 us
  transfers between devices with their start and end apart: 9 -> 9, of which waited for: 9 -> 9; matrix products, arithmetic and copies ran while one was open for 5% -> 6% of each run, Pallas kernels for 0% -> 0%
where the time goes in v1:
time: 739 us; the launch traced here: 732 us
  waiting for transfers between devices  421 us (57%)
  matrix products  94.3 us (13%)
  Pallas kernels  75.5 us (10%)
  blocking collectives  65.2 us (9%)
  other arithmetic  35.3 us (5%)
  local copies, waits for them, and re-layouts  24.1 us (3%)
  between operations  15 us (2%)
    psum x1, waiting for transfers between devices, per_device(): lax.psum(query_weight_grad.astype(jnp.bfloat16), 'dp').astype(jnp.float32)  137 us
    reduce_scatter x1, waiting for transfers between devices, per_device(): lax.psum_scatter(contract_cols(lax.slice_in_dim(pre_grad, 0, local_rows *...  44.7 us
    reduce_scatter x1, waiting for transfers between devices, per_device(): lax.psum_scatter(jnp.dot(lax.slice_in_dim(attended, 0, local_rows * lax.a...  44 us
    reduce_scatter x1, waiting for transfers between devices, per_device(): lax.psum_scatter(jnp.dot(lax.slice_in_dim(act_low, 0, local_rows * lax.ax...  44 us
    psum x1, blocking collectives, per_device(): lax.psum((out_bias_grad, first_gain_grad, first_shift_grad, down_bias_gra...  43.5 us
    pallas_call x1, Pallas kernels, attention_backward(): pl.pallas_call(partial(backward_kernel, heads), grid=grid, in_specs=[e_sp...  42.2 us
    all_gather x1, waiting for transfers between devices, per_device(): hidden_all = lax.all_gather(hidden_low, 'mp', axis=0, tiled=True)  34.4 us
    all_gather x1, waiting for transfers between devices, per_device(): row_piece = lax.all_gather(branch_two_low, 'mp', axis=0, tiled=True)  34.4 us
  transfers between devices with their start and end apart: 9, of which 9 were waited for; matrix products, arithmetic and copies ran while one was open for 6% of the time, Pallas kernels for 0%

profile of v1, /device:TPU:0, one launch (start us, length us, event | category | flops | bytes accessed | tf_op | source)
XLA Modules:
  0.0 731.9 jit_solution(6629792520796658668)
XLA Ops:
  15.7 31.1 %all-gather.5.cloned.1.call-done = bf16[2048,1024]{1,0:T(8,128)(2,1)} async-done(((bf16[512,1024]{1,0:T(8,128)(2,1)}), bf16[2048,1024]{1,0:T(8,128)(2,1)}) %all-gather.5.cloned.1.call-update) | async-done | bytes 4194320 | tf_op jit(solution)/shard_map/all_gather | solution.py:258
  46.8 5.6 convolution_bitcast_fusion
  56.3 33.4 %attention_forward.1 = (bf16[4,2048,2048]{2,1,0:T(8,128)(2,1)}, bf16[2048,256]{1,0:T(8,128)(2,1)}, f32[4,1,2048]{2,1,0:T(1,128)}) custom-call(s32[1]{0:T(128)} %bitcast.30.len_ref, bf16[2048,256]{1,0:T(8,128)(2,1)} %get-tuple-element.81.q_ref, bf16[2048,256]{1,0:T(8,128)(2,1)} %slice.41.k_ref, bf16[256,2048]{1,0:T(8,128)(2,1)} %copy.36.vt_ref), custom_call_target="tpu_custom_call" | custom-call | tf_op jit(solution)/shard_map/attention_forward/pallas_call | solution.py:166
  89.7 4.6 convolution_convert_fusion
  95.0 44.0 %reduce-scatter.5.cloned.1.call-done = bf16[512,1024]{1,0:T(8,128)(2,1)} async-done(((bf16[2048,1024]{1,0:T(8,128)(2,1)}), bf16[512,1024]{1,0:T(8,128)(2,1)}) %reduce-scatter.5.cloned.1.call-update) | async-done | bytes 1048592 | tf_op jit(solution)/shard_map/reduce_scatter | solution.py:263
  144.4 34.4 %all-gather.7.cloned.1.call-done = bf16[2048,1024]{1,0:T(8,128)(2,1)} async-done(((bf16[512,1024]{1,0:T(8,128)(2,1)}), bf16[2048,1024]{1,0:T(8,128)(2,1)}) %all-gather.7.cloned.1.call-update) | async-done | bytes 4194320 | tf_op jit(solution)/shard_map/all_gather | solution.py:277
  178.8 25.4 %multiply_convert_fusion = (bf16[2048,1024]{1,0:T(8,128)(2,1)S(1)}, f32[2048,1024]{1,0:T(8,128)}, f32[2048,1024]{1,0:T(8,128)}) fusion(f32[1024]{0:T(1024)S(1)} %convert_element_type.146, bf16[2048,1024]{1,0:T(8,128)(2,1)} %all-gather.7.cloned.1.call-done, bf16[1024,1024]{1,0:T(8,128)(2,1)S(1)} %copy-done), kind=kOutput, calls=%fused_computation.3 | convolution fusion | flops 4433379328 | bytes 27267072 | tf_op jit(solution)/shard_map/dot_general | solution.py:278
  206.1 6.0 convolution_convert_fusion.3
  212.9 44.0 %reduce-scatter.7.cloned.1.call-done = bf16[512,1024]{1,0:T(8,128)(2,1)} async-done(((bf16[2048,1024]{1,0:T(8,128)(2,1)}), bf16[512,1024]{1,0:T(8,128)(2,1)}) %reduce-scatter.7.cloned.1.call-update) | async-done | bytes 1048592 | tf_op jit(solution)/shard_map/reduce_scatter | solution.py:280
  256.9 2.6 fusion.23
  260.9 2.9 fusion.21
  264.1 34.4 %all-gather.9.cloned.1.call-done = bf16[2048,1024]{1,0:T(8,128)(2,1)} async-done(((bf16[512,1024]{1,0:T(8,128)(2,1)}), bf16[2048,1024]{1,0:T(8,128)(2,1)}) %all-gather.9.cloned.1.call-update) | async-done | bytes 4194320 | tf_op jit(solution)/shard_map/all_gather | solution.py:298
  298.4 13.3 %fusion.20 = (bf16[1024]{0:T(1024)(128)(2,1)S(1)}, bf16[2048,1024]{1,0:T(8,128)(2,1)S(1)}) fusion(f32[2048,1024]{1,0:T(8,128)} %get-tuple-element.79, f32[2048,1024]{1,0:T(8,128)} %get-tuple-element.90, f32[1024]{0:T(1024)S(1)} %convert_element_type.146, bf16[2048,1024]{1,0:T(8,128)(2,1)} %all-gather.9.cloned.1.call-done, bf16[1024,1024]{1,0:T(8,128)(2,1)} %param.31), kind=kOutput, calls=%fused_computation.75 | convolution fusion | flops 4328520704 | bytes 27269120 | tf_op jit(solution)/shard_map/dot_general | solution.py:222
  313.7 6.2 convolution_convert_fusion.2
  320.0 44.7 %reduce-scatter.9.cloned.1.call-done = bf16[512,1024]{1,0:T(8,128)(2,1)} async-done(((bf16[2048,1024]{1,0:T(8,128)(2,1)}), bf16[512,1024]{1,0:T(8,128)(2,1)}) %reduce-scatter.9.cloned.1.call-update) | async-done | bytes 1048592 | tf_op jit(solution)/shard_map/reduce_scatter | solution.py:312
  364.7 3.7 multiply_reduce_fusion
  372.5 9.5 %convolution_convert_fusion.5 = bf16[1024,1024]{1,0:T(8,128)(2,1)} fusion(bf16[2048,1024]{1,0:T(8,128)(2,1)} %copy-done.26, bf16[2048,1024]{1,0:T(8,128)(2,1)} %all-gather.9.cloned.1.call-done), kind=kOutput, calls=%fused_computation.51 | convolution fusion | flops 4296015872 | bytes 10485760 | tf_op jit(solution)/shard_map/dot_general | solution.py:216
  382.0 5.8 convolution_convert_fusion.6
  387.8 18.9 %all-gather.11.cloned.1.call-done = bf16[2048,1024]{1,0:T(8,128)(2,1)} async-done(((bf16[512,1024]{1,0:T(8,128)(2,1)}), bf16[2048,1024]{1,0:T(8,128)(2,1)}) %all-gather.11.cloned.1.call-update) | async-done | bytes 4194320 | tf_op jit(solution)/shard_map/all_gather | solution.py:326
  406.7 4.5 convolution_convert_fusion.4.g_ref
  411.1 42.2 %attention_backward.1 = (bf16[2048,256]{1,0:T(8,128)(2,1)}, bf16[2048,256]{1,0:T(8,128)(2,1)}, bf16[2048,256]{1,0:T(8,128)(2,1)}) custom-call(bf16[4,2048,2048]{2,1,0:T(8,128)(2,1)} %get-tuple-element.24.e_ref, f32[4,1,2048]{2,1,0:T(1,128)} %get-tuple-element.25.r_ref, bf16[2048,256]{1,0:T(8,128)(2,1)} %get-tuple-element.81.q_ref, ...), custom_call_target="tpu_custom_call" | custom-call | tf_op jit(solution)/shard_map/attention_backward/pallas_call | solution.py:197
  456.9 3.5 fusion.17
  463.8 7.8 %convolution_convert_fusion.1 = bf16[2048,1024]{1,0:T(8,128)(2,1)} fusion(bf16[2048,768]{1,0:T(8,128)(2,1)} %copy-done.14, bf16[1024,768]{1,0:T(8,128)(2,1)} %constant_dynamic-update-slice_fusion), kind=kOutput, calls=%fused_computation.19 | convolution fusion | flops 3223322624 | bytes 8912896 | tf_op jit(solution)/shard_map/dot_general | solution.py:222
  471.5 43.5 %all-reduce = (f32[1024]{0:T(1024)}, f32[1024]{0:T(1024)}, f32[1024]{0:T(1024)}, f32[1024]{0:T(1024)}, f32[1024]{0:T(1024)}, /*index=5*/f32[1024]{0:T(1024)}) all-reduce(f32[1024]{0:T(1024)S(1)} %get-tuple-element.70, f32[1024]{0:T(1024)S(1)} %get-tuple-element.46, ...), channel_id=1, replica_groups=mesh['dp'=8,'mp'=4] {'dp','mp'}, use_global_device_ids=true, to_apply=%region_21.0 | all-reduce | flops 6144 | bytes 49152 | tf_op jit(solution)/shard_map/psum | solution.py:385
  515.0 21.7 %all-reduce.1 = (bf16[256]{0:T(256)(128)(2,1)S(1)}, bf16[256]{0:T(256)(128)(2,1)S(1)}, bf16[1024]{0:T(1024)(128)(2,1)S(1)}) all-reduce(bf16[256]{0:T(256)(128)(2,1)S(1)} %get-tuple-element.88, bf16[256]{0:T(256)(128)(2,1)S(1)} %get-tuple-element.86, bf16[1024]{0:T(1024)(128)(2,1)S(1)} %get-tuple-element.72), channel_id=1, replica_groups=mesh['dp'=8,'mp'=4] {'dp'}, use_global_device_ids=true, to_apply=%region_14.0 | all-reduce | flops 1536 | bytes 6144 | tf_op jit(solution)/shard_map/psum | solution.py:369
  538.5 137.5 %all-reduce.5.cloned.1.call-done = (bf16[1024,256]{0,1:T(8,128)(2,1)}, bf16[1024,256]{0,1:T(8,128)(2,1)}, bf16[1024,256]{0,1:T(8,128)(2,1)}, bf16[256,1024]{1,0:...) async-done(((bf16[1024,256]{0,1:T(8,128)(2,1)}, bf16[1024,256]{0,1:T(8,128)(2,1)}, bf16[1024,256]{0,1:T(8,128)(2,1)}, bf16[256,1024]{1,0:T(8,128)(2,1)}, ...) | async-done | bytes 6291472 | tf_op jit(solution)/shard_map/psum | solution.py:368
  676.0 2.3 copy.37
  678.2 2.2 copy.38
  683.8 4.1 convert_element_type.172
  687.9 2.5 convert_element_type.175
  690.3 31.7 %reduce-scatter.11.cloned.1.call-done = bf16[512,1024]{1,0:T(8,128)(2,1)} async-done(((bf16[2048,1024]{1,0:T(8,128)(2,1)}), bf16[512,1024]{1,0:T(8,128)(2,1)}) %reduce-scatter.11.cloned.1.call-update) | async-done | bytes 1048592 | tf_op jit(solution)/shard_map/reduce_scatter | solution.py:345
  722.1 3.2 add_convert_fusion.1
  (115 shorter events, 39.9 us)
Async XLA Ops:
  7.2 171.6 %copy-start = (bf16[1024,1024]{1,0:T(8,128)(2,1)S(1)}, bf16[1024,1024]{1,0:T(8,128)(2,1)}, u32[]{:S(2)}) copy-start(bf16[1024,1024]{1,0:T(8,128)(2,1)} %param.29) | copy-start | bytes 6291460
  7.2 39.6 %all-gather.5.cloned.1.call-start = ((), (), s32[]{:S(2)}) async-start(), calls=%async_computation.4 | async-start | bytes 5242880 | tf_op jit(solution)/shard_map/all_gather | solution.py:258
  7.9 131.1 %reduce-scatter.5.cloned.1.call-start = ((), (), s32[]{:S(2)}) async-start(), calls=%async_computation.5 | async-start | bytes 5242880 | tf_op jit(solution)/shard_map/reduce_scatter | solution.py:263
  54.9 34.8 %copy-start.6 = (bf16[2048,256]{1,0:T(8,128)(2,1)}, bf16[2048,256]{1,0:T(8,128)(2,1)S(1)}, u32[]{:S(2)}) copy-start(bf16[2048,256]{1,0:T(8,128)(2,1)S(1)} %get-tuple-element.80.v_ref) | copy-start | bytes 3145732
  94.3 44.8 %copy-start.1 = (bf16[512,1024]{1,0:T(8,128)(2,1)S(1)}, bf16[512,1024]{1,0:T(8,128)(2,1)}, u32[]{:S(2)}) copy-start(bf16[512,1024]{1,0:T(8,128)(2,1)} %param.18) | copy-start | bytes 3145732
  94.3 84.5 %all-gather.7.cloned.1.call-start = ((), (), s32[]{:S(2)}) async-start(), calls=%async_computation.6 | async-start | bytes 5242880 | tf_op jit(solution)/shard_map/all_gather | solution.py:277
  95.0 49.4 %copy-start.18 = (bf16[1024]{0:T(1024)(128)(2,1)S(1)}, bf16[1024]{0:T(1024)(128)(2,1)}, u32[]{:S(2)}) copy-start(bf16[1024]{0:T(1024)(128)(2,1)} %param.30) | copy-start | bytes 6148
  139.1 3.5 copy-start.2
  144.2 112.7 %reduce-scatter.7.cloned.1.call-start = ((), (), s32[]{:S(2)}) async-start(), calls=%async_computation.7 | async-start | bytes 5242880 | tf_op jit(solution)/shard_map/reduce_scatter | solution.py:280
  178.8 27.3 %copy-start.25 = (bf16[1024,1024]{1,0:T(8,128)(2,1)S(1)}, bf16[1024,1024]{1,0:T(8,128)(2,1)}, u32[]{:S(2)}) copy-start(bf16[1024,1024]{1,0:T(8,128)(2,1)} %param.31) | copy-start | bytes 6291460
  204.2 1.9 copy-start.26
  212.2 86.2 %all-gather.9.cloned.1.call-start = ((), (), s32[]{:S(2)}) async-start(), calls=%async_computation.8 | async-start | bytes 5242880 | tf_op jit(solution)/shard_map/all_gather | solution.py:298
  256.9 3.0 copy-start.8
  263.8 100.9 %reduce-scatter.9.cloned.1.call-start = ((), (), s32[]{:S(2)}) async-start(), calls=%async_computation.9 | async-start | bytes 5242880 | tf_op jit(solution)/shard_map/reduce_scatter | solution.py:312
  311.7 2.0 copy-start.27
  320.0 86.7 %all-gather.11.cloned.1.call-start = ((), (), s32[]{:S(2)}) async-start(), calls=%async_computation.10 | async-start | bytes 5242880 | tf_op jit(solution)/shard_map/all_gather | solution.py:326
  364.7 3.8 copy-start.3
  364.7 3.8 copy-start.4
  364.7 3.8 copy-start.9
  369.6 1.3 copy-start.5
  372.0 303.9 %all-reduce.5.cloned.1.call-start = ((), (), s32[]{:S(2)}) async-start(), calls=%async_computation.12 | async-start | bytes 12582912 | tf_op jit(solution)/shard_map/psum | solution.py:368
  372.5 9.5 %copy-start.23 = (bf16[2048,1024]{1,0:T(8,128)(2,1)S(1)}, bf16[2048,1024]{1,0:T(8,128)(2,1)}, u32[]{:S(2)}) copy-start(bf16[2048,1024]{1,0:T(8,128)(2,1)} %all-gather.7.cloned.1.call-done) | copy-start | bytes 12582916
  372.5 9.5 %copy-start.28 = (bf16[2048,1024]{1,0:T(8,128)(2,1)S(1)}, bf16[2048,1024]{1,0:T(8,128)(2,1)}, u32[]{:S(2)}) copy-start(bf16[2048,1024]{1,0:T(8,128)(2,1)} %copy-done.27) | copy-start | bytes 12582916
  382.0 24.6 %copy-start.12 = (bf16[256,1024]{1,0:T(8,128)(2,1)S(1)}, bf16[256,1024]{1,0:T(8,128)(2,1)}, u32[]{:S(2)}) copy-start(bf16[256,1024]{1,0:T(8,128)(2,1)} %param.25) | copy-start | bytes 1572868
  453.3 3.2 copy-start.11
  453.3 3.6 copy-start.22
  456.9 3.6 copy-start.14
  456.9 4.7 copy-start.7
  456.9 4.7 copy-start.24
  463.7 258.4 %reduce-scatter.11.cloned.1.call-start = ((), (), s32[]{:S(2)}) async-start(), calls=%async_computation.11 | async-start | bytes 5242880 | tf_op jit(solution)/shard_map/reduce_scatter | solution.py:345
  676.0 6.7 copy-start.13
  682.7 5.2 copy-start.10
  (6 other events, 4.2 us)
Sparse Core Ops, SparseCore 0:
  9.6 37.1 all-gather.4
  94.5 44.5 reduce-scatter.4
  144.3 34.4 all-gather.6
  212.3 44.5 reduce-scatter.6
  263.9 34.4 all-gather.8
  320.1 44.5 reduce-scatter.8
  372.2 34.4 all-gather.10
  463.8 212.0 all-reduce.4
  678.5 43.5 reduce-scatter.10

commit v2 on v1

--- a/solution.py
+++ b/solution.py
@@ -231,7 +231,7 @@
     return (query_part, key_part, value_part)
 
 
-def per_device(
+def per_device_general(
     tokens,
     lengths,
     query_weight,
@@ -414,6 +414,815 @@
     )
 
 
+MESH = pl.DeviceIdType.MESH
+VMEM_BYTES = 63 * 1024 * 1024
+CHUNKS = 4
+
+
+def flip(index, bit):
+    low = index // bit % 2
+    return index + bit * (1 - 2 * low)
+
+
+def mp_peer(relation):
+    dp, mp = lax.axis_index("dp"), lax.axis_index("mp")
+    for bit in (1, 2):
+        if relation // bit % 2:
+            mp = flip(mp, bit)
+    return (dp, mp)
+
+
+def dp_peer(bit):
+    return (flip(lax.axis_index("dp"), bit), lax.axis_index("mp"))
+
+
+def greet(peers):
+    barrier = pltpu.get_barrier_semaphore()
+    for device in peers:
+        pl.semaphore_signal(barrier, inc=1, device_id=device, device_id_type=MESH)
+    pl.semaphore_wait(barrier, len(peers))
+
+
+def remote(src, dst, send, recv, device):
+    return pltpu.make_async_remote_copy(
+        src_ref=src, dst_ref=dst, send_sem=send, recv_sem=recv, device_id=device, device_id_type=MESH
+    )
+
+
+def repeat(count, body):
+    def step(i, carry):
+        body(i)
+        return carry
+
+    lax.fori_loop(0, count, step, 0)
+
+
+class Gather:
+    def __init__(self, own, land, send, recv, chunks=CHUNKS):
+        self.own, self.land, self.send, self.recv, self.chunks = own, land, send, recv, chunks
+        self.size = own.shape[0] // chunks
+
+    def copy(self, relation, j):
+        rows = pl.ds(j * self.size, self.size)
+        src = self.land.at[1, rows] if relation == 3 else self.own.at[rows]
+        return remote(
+            src,
+            self.land.at[relation - 1, rows],
+            self.send.at[relation - 1, j],
+            self.recv.at[relation - 1, j],
+            mp_peer(2 if relation == 2 else 1),
+        )
+
+    def start(self, j):
+        self.copy(2, j).start()
+        self.copy(1, j).start()
+
+    def arrive(self, relation, j):
+        self.copy(relation, j).wait_recv()
+        if relation == 2:
+            self.copy(3, j).start()
+
+    def drain(self):
+        def body(j):
+            for relation in (1, 2, 3):
+                self.copy(relation, j).wait_send()
+
+        repeat(self.chunks, body)
+
+
+PAIR, FAR, NEAR = 0, 1, 2
+
+
+class Reduce:
+    def __init__(self, out, land, send, recv, chunks=CHUNKS):
+        self.out, self.land, self.send, self.recv, self.chunks = out, land, send, recv, chunks
+        self.size = out.shape[1] // chunks
+
+    def copy(self, kind, j):
+        rows = pl.ds(j * self.size, self.size)
+        return remote(
+            self.out.at[kind, rows],
+            self.land.at[kind, rows],
+            self.send.at[kind, j],
+            self.recv.at[kind, j],
+            mp_peer(2 if kind == FAR else 1),
+        )
+
+    def post(self, kind, j, value):
+        self.out[kind, pl.ds(j * self.size, self.size)] = value.astype(BF)
+        self.copy(kind, j).start()
+
+    def forward_pair(self, j, mine):
+        self.copy(PAIR, j).wait_recv()
+        rows = pl.ds(j * self.size, self.size)
+        self.post(FAR, j, mine + self.land[PAIR, rows].astype(F32))
+
+    def total(self, j, mine):
+        self.copy(NEAR, j).wait_recv()
+        self.copy(FAR, j).wait_recv()
+        rows = pl.ds(j * self.size, self.size)
+        return mine + self.land[NEAR, rows].astype(F32) + self.land[FAR, rows].astype(F32)
+
+    def drain(self):
+        def body(j):
+            for kind in (PAIR, FAR, NEAR):
+                self.copy(kind, j).wait_send()
+
+        repeat(self.chunks, body)
+
+
+def transfer_sems(chunks=CHUNKS):
+    return [pltpu.SemaphoreType.DMA((3, chunks)), pltpu.SemaphoreType.DMA((3, chunks))]
+
+
+def comm_params(collective_id):
+    return pltpu.CompilerParams(
+        collective_id=collective_id, has_side_effects=True, vmem_limit_bytes=VMEM_BYTES
+    )
+
+
+WHOLE = pl.BlockSpec(memory_space=pltpu.VMEM)
+
+
+def shaped(*shape, dtype=None):
+    return jax.ShapeDtypeStruct(shape, dtype or BF)
+
+
+def column_sum(value):
+    return jnp.sum(value, 0, keepdims=True)
+
+
+def row_mean(value):
+    return jnp.mean(value, -1, keepdims=True)
+
+
+def project_kernel(
+    x_ref, wq_ref, wk_ref, wv_ref, qb_ref, vb_ref, q_ref, k_ref, v_ref, vt_ref, all_ref, land, send, recv, save
+):
+    rows_here = x_ref.shape[0]
+    greet([mp_peer(1), mp_peer(2)])
+    gather = Gather(x_ref, land, send, recv)
+    repeat(CHUNKS, gather.start)
+    size = gather.size
+
+    def emit(x, at):
+        rows = pl.ds(at, x.shape[0])
+        q = (mm(x, wq_ref[...], 1, 0) + qb_ref[...]).astype(BF)
+        q_ref[rows] = (q.astype(F32) * HD**-0.5).astype(BF)
+        k_ref[rows] = mm(x, wk_ref[...], 1, 0).astype(BF)
+        v = mm(x, wv_ref[...], 1, 0) + vb_ref[...]
+        v_ref[rows] = v.astype(BF)
+        vt_ref[:, rows] = v.T.astype(BF)
+
+    stores = [pltpu.make_async_copy(x_ref, all_ref.at[0], save.at[0])]
+    stores[0].start()
+    for i in range(2):
+        emit(x_ref[pl.ds(i * 2 * size, 2 * size)], i * 2 * size)
+    for i in range(2):
+        gather.arrive(1, 2 * i)
+        gather.arrive(1, 2 * i + 1)
+        emit(land[0, pl.ds(i * 2 * size, 2 * size)], rows_here + i * 2 * size)
+    for j in range(CHUNKS):
+        gather.arrive(2, j)
+        gather.arrive(3, j)
+        for s in (2, 3):
+            emit(land[s - 1, pl.ds(j * size, size)], s * rows_here + j * size)
+    for s in (1, 2, 3):
+        stores.append(pltpu.make_async_copy(land.at[s - 1], all_ref.at[s], save.at[s]))
+        stores[-1].start()
+    gather.drain()
+    for store in stores:
+        store.wait()
+
+
+def gather_project(tokens, wq, wk, wv, q_bias, v_bias):
+    rows, width = tokens.shape
+    cols = wq.shape[1]
+    return pl.pallas_call(
+        project_kernel,
+        in_specs=[WHOLE] * 6,
+        out_specs=[WHOLE] * 4 + [pl.BlockSpec(memory_space=pl.ANY)],
+        out_shape=[shaped(4 * rows, cols)] * 3 + [shaped(cols, 4 * rows), shaped(4, rows, width)],
+        scratch_shapes=[
+            pltpu.VMEM((3, rows, width), BF),
+            *transfer_sems(),
+            pltpu.SemaphoreType.DMA((4,)),
+        ],
+        name="gather_project",
+        compiler_params=comm_params(0),
+    )(tokens, wq, wk, wv, q_bias, v_bias)
+
+
+HALVES = 2
+
+
+def forward_order(step):
+    far = 2 * (3 - step % 2) + step // 2
+    near = 2 * (1 - (step - 4) // 2) + step % 2
+    return jnp.where(step < 4, far, near)
+
+
+def attend_kernel(
+    q_ref, k_ref, vt_ref, bias_ref, w_ref, x_ref, vec_ref,
+    e_ref, o_ref, r_ref, n_ref, i_ref, h_ref,
+    k_aug, v_aug, out, land, mine, pending, send, recv,
+):
+    step = pl.program_id(0)
+    seq_len, block = k_ref.shape[0], q_ref.shape[0]
+    pairs = k_ref.shape[1] // WIDE
+    reduce = Reduce(out, land, send, recv, HALVES)
+
+    @pl.when(step == 0)
+    def _():
+        greet([mp_peer(1), mp_peer(2)])
+        lanes = lax.broadcasted_iota(jnp.int32, (seq_len, WIDE), 1)
+        for p in range(pairs):
+            keys = k_ref[:, p * WIDE : (p + 1) * WIDE].astype(F32)
+            for h in range(2):
+                other = (1 - h) * HD
+                k_aug[2 * p + h] = jnp.where(
+                    lanes // HD == h, keys, jnp.where(lanes == other, bias_ref[...], 0.0)
+                ).astype(BF)
+                at = (2 * p + h) * HD
+                v_aug[2 * p + h, :HD] = vt_ref[at : at + HD, :]
+                v_aug[2 * p + h, HD:] = jnp.ones((16, seq_len), BF)
+
+    lanes = lax.broadcasted_iota(jnp.int32, (block, WIDE), 1)
+    outs = []
+    for p in range(pairs):
+        query = q_ref[:, p * WIDE : (p + 1) * WIDE].astype(F32)
+        scores = []
+        for h in range(2):
+            other = (1 - h) * HD
+            q_aug = jnp.where(
+                lanes // HD == h, query, jnp.where(lanes == other, 1.0, 0.0)
+            ).astype(BF)
+            scores.append(mm(k_aug[2 * p + h], q_aug, 1, 1))
+        for h in range(2):
+            top = jnp.max(scores[h], 0, keepdims=True)
+            expon = jnp.exp(scores[h] - top).astype(BF)
+            e_ref[0, 2 * p + h] = expon
+            total = mm(v_aug[2 * p + h], expon, 1, 0)
+            inverse = 1.0 / total[HD : HD + 1]
+            r_ref[0, 2 * p + h] = inverse
+            outs.append(total[:HD] * inverse)
+    attended = jnp.concatenate(outs, 0).T.astype(BF)
+    o_ref[...] = attended
+    partial_rows = mm(attended, w_ref[...], 1, 0)
+
+    for t in range(4 * HALVES):
+
+        @pl.when(step == t)
+        def _(t=t):
+            if t < 4 and t % 2 == 0:
+                reduce.post(PAIR, t // 2, partial_rows)
+            elif t < 4:
+                pending[...] = partial_rows
+                reduce.forward_pair(t // 2, pending[...])
+            elif t < 6:
+                reduce.post(NEAR, t - 4, partial_rows)
+            else:
+                mine[pl.ds((t - 6) * block, block)] = partial_rows
+
+    @pl.when(step == 4 * HALVES - 1)
+    def _():
+        for j in range(HALVES):
+            rows = pl.ds(j * block, block)
+            resid = x_ref[rows].astype(F32) + reduce.total(j, mine[rows]) + vec_ref[0:1]
+            center = resid - row_mean(resid)
+            inv_std = lax.rsqrt(row_mean(center * center) + epsilon)
+            normed = center * inv_std
+            n_ref[rows] = normed
+            i_ref[rows] = inv_std
+            h_ref[rows] = (normed * vec_ref[1:2] + vec_ref[2:3]).astype(BF)
+        reduce.drain()
+
+
+def attend(q, k, vt, bias, out_weight, tokens, vectors):
+    all_rows, cols = q.shape
+    rows, width = tokens.shape
+    block = rows // HALVES
+    heads = cols // HD
+    steps = all_rows // block
+
+    def fixed(*shape):
+        return pl.BlockSpec(shape, lambda i: (0,) * len(shape))
+
+    return pl.pallas_call(
+        attend_kernel,
+        grid=(steps,),
+        in_specs=[
+            pl.BlockSpec((block, cols), lambda i: (forward_order(i), 0)),
+            fixed(all_rows, cols),
+            fixed(cols, all_rows),
+            fixed(all_rows, 1),
+            fixed(cols, width),
+            fixed(rows, width),
+            fixed(*vectors.shape),
+        ],
+        out_specs=[
+            pl.BlockSpec((1, heads, all_rows, block), lambda i: (forward_order(i), 0, 0, 0)),
+            pl.BlockSpec((block, cols), lambda i: (forward_order(i), 0)),
+            pl.BlockSpec((1, heads, 1, block), lambda i: (forward_order(i), 0, 0, 0)),
+            fixed(rows, width),
+            fixed(rows, 1),
+            fixed(rows, width),
+        ],
+        out_shape=[
+            shaped(steps, heads, all_rows, block),
+            shaped(all_rows, cols),
+            shaped(steps, heads, 1, block, dtype=F32),
+            shaped(rows, width, dtype=F32),
+            shaped(rows, 1, dtype=F32),
+            shaped(rows, width),
+        ],
+        scratch_shapes=[
+            pltpu.VMEM((heads, all_rows, WIDE), BF),
+            pltpu.VMEM((heads, HD + 16, all_rows), BF),
+            pltpu.VMEM((3, rows, width), BF),
+            pltpu.VMEM((3, rows, width), BF),
+            pltpu.VMEM((rows, width), F32),
+            pltpu.VMEM((block, width), F32),
+            *transfer_sems(HALVES),
+        ],
+        name="attend",
+        compiler_params=comm_params(1),
+    )(q, k, vt, bias, out_weight, tokens, vectors)
+
+
+ROOT_HALF = 0.7071067811865476
+ROOT_TAU = 0.3989422804014327
+
+
+def feed_forward_kernel(
+    h_ref, n_ref, i_ref, g_ref, up_ref, ub_ref, down_ref, vec_ref,
+    out_ref, b1_ref, r1_ref, upg_ref, downg_ref, ubg_ref, small_ref,
+    land_h, act, slope, branch, land_b, out1, land1, out2, land2, mine, pending, r2,
+    gs1, gr1, gs2, gr2, rs1, rr1, rs2, rr2,
+):
+    rows_here, width = h_ref.shape
+    size = rows_here // CHUNKS
+    first_gain, first_shift, down_bias, second_gain, second_shift = (vec_ref[i : i + 1] for i in range(5))
+    greet([mp_peer(1), mp_peer(2)])
+    gather1, gather2 = Gather(h_ref, land_h, gs1, gr1), Gather(branch, land_b, gs2, gr2)
+    reduce1, reduce2 = Reduce(out1, land1, rs1, rr1), Reduce(out2, land2, rs2, rr2)
+    repeat(CHUNKS, gather1.start)
+    small_ref[...] = jnp.zeros_like(small_ref)
+    ubg_ref[...] = jnp.zeros_like(ubg_ref)
+
+    def forward(x):
+        pre = mm(x, up_ref[...], 1, 0) + ub_ref[...]
+        cdf = 0.5 + 0.5 * lax.erf(pre * ROOT_HALF)
+        active = (pre * cdf).astype(BF)
+        steep = (cdf + pre * jnp.exp(-0.5 * pre * pre) * ROOT_TAU).astype(BF)
+        return active, steep, mm(active, down_ref[...], 1, 0)
+
+    def backward(grad, steep):
+        pre_grad = (mm(grad, down_ref[...], 1, 1) * steep.astype(F32)).astype(BF)
+        ubg_ref[...] += column_sum(pre_grad.astype(F32))
+        return pre_grad, mm(pre_grad, up_ref[...], 1, 1)
+
+    def chunk_rows(j):
+        return pl.ds(pl.multiple_of(j * size, size), size)
+
+    def double_rows(j):
+        return pl.ds(pl.multiple_of(j * 2 * size, 2 * size), 2 * size)
+
+    def halves(value):
+        return value[:size], value[size:]
+
+    def own_forward(i):
+        rows = double_rows(i)
+        act[0, rows], slope[0, rows], mine[rows] = forward(h_ref[rows])
+
+    def near_forward(i):
+        gather1.arrive(1, 2 * i)
+        gather1.arrive(1, 2 * i + 1)
+        rows = double_rows(i)
+        act[1, rows], slope[1, rows], part = forward(land_h[0, rows])
+        for k, half in enumerate(halves(part)):
+            reduce1.post(NEAR, 2 * i + k, half)
+
+    def far_forward(j):
+        gather1.arrive(2, j)
+        gather1.arrive(3, j)
+        rows = chunk_rows(j)
+        active, steep, part = forward(jnp.concatenate([land_h[1, rows], land_h[2, rows]], 0))
+        for s in (2, 3):
+            act[s, rows] = halves(active)[s - 2]
+            slope[s, rows] = halves(steep)[s - 2]
+        pending[rows] = part[:size]
+        reduce1.post(PAIR, j, part[size:])
+
+        @pl.when(j > 0)
+        def _():
+            reduce1.forward_pair(j - 1, pending[chunk_rows(j - 1)])
+
+    repeat(2, own_forward)
+    repeat(2, near_forward)
+    repeat(CHUNKS, far_forward)
+    reduce1.forward_pair(CHUNKS - 1, pending[chunk_rows(CHUNKS - 1)])
+
+    def second_norm(j):
+        rows = chunk_rows(j)
+        hidden = n_ref[rows] * first_gain + first_shift
+        resid = hidden + reduce1.total(j, mine[rows]) + down_bias
+        center = resid - row_mean(resid)
+        inv_std = lax.rsqrt(row_mean(center * center) + epsilon)
+        normed = center * inv_std
+        out_ref[rows] = (normed * second_gain + second_shift).astype(BF)
+        grad = g_ref[rows].astype(F32)
+        product = grad * normed
+        small_ref[0:1] += column_sum(product)
+        small_ref[1:2] += column_sum(grad)
+        scaled = grad * second_gain
+        back = inv_std * (scaled - row_mean(scaled) - normed * row_mean(scaled * normed))
+        small_ref[2:3] += column_sum(back)
+        r2[rows] = back
+        branch[rows] = back.astype(BF)
+        gather2.start(j)
+
+    repeat(CHUNKS, second_norm)
+
+    def own_backward(i):
+        rows = double_rows(i)
+        slope[0, rows], mine[rows] = backward(branch[rows], slope[0, rows])
+
+    def near_backward(i):
+        gather2.arrive(1, 2 * i)
+        gather2.arrive(1, 2 * i + 1)
+        rows = double_rows(i)
+        slope[1, rows], part = backward(land_b[0, rows], slope[1, rows])
+        for k, half in enumerate(halves(part)):
+            reduce2.post(NEAR, 2 * i + k, half)
+
+    def far_backward(j):
+        gather2.arrive(2, j)
+        gather2.arrive(3, j)
+        rows = chunk_rows(j)
+        pre_grad, part = backward(
+            jnp.concatenate([land_b[1, rows], land_b[2, rows]], 0),
+            jnp.concatenate([slope[2, rows], slope[3, rows]], 0),
+        )
+        for s in (2, 3):
+            slope[s, rows] = halves(pre_grad)[s - 2]
+        pending[rows] = part[:size]
+        reduce2.post(PAIR, j, part[size:])
+
+        @pl.when(j > 0)
+        def _():
+            reduce2.forward_pair(j - 1, pending[chunk_rows(j - 1)])
+
+    repeat(2, own_backward)
+    repeat(2, near_backward)
+    repeat(CHUNKS, far_backward)
+    reduce2.forward_pair(CHUNKS - 1, pending[chunk_rows(CHUNKS - 1)])
+
+    tile = 256
+
+    def down_grad(t):
+        cols = pl.ds(pl.multiple_of(t * tile, tile), tile)
+        total = mm(act[0, :, cols], branch[...], 0, 0)
+        for s in (1, 2, 3):
+            total += mm(act[s, :, cols], land_b[s - 1], 0, 0)
+        downg_ref[cols] = total.astype(BF)
+
+    def up_grad(t):
+        cols = pl.ds(pl.multiple_of(t * tile, tile), tile)
+        total = mm(h_ref[:, cols], slope[0], 0, 0)
+        for s in (1, 2, 3):
+            total += mm(land_h[s - 1, :, cols], slope[s], 0, 0)
+        upg_ref[cols] = total.astype(BF)
+
+    repeat(down_ref.shape[0] // tile, down_grad)
+    repeat(width // tile, up_grad)
+
+    def first_norm(j):
+        rows = chunk_rows(j)
+        normed = n_ref[rows]
+        grad = r2[rows] + reduce2.total(j, mine[rows])
+        small_ref[3:4] += column_sum(grad * normed)
+        small_ref[4:5] += column_sum(grad)
+        scaled = grad * first_gain
+        back = i_ref[rows] * (scaled - row_mean(scaled) - normed * row_mean(scaled * normed))
+        small_ref[5:6] += column_sum(back)
+        r1_ref[rows] = back
+        b1_ref[rows] = back.astype(BF)
+
+    repeat(CHUNKS, first_norm)
+    for transfer in (gather1, gather2, reduce1, reduce2):
+        transfer.drain()
+
+
+def feed_forward(hidden, normed, inv_std, output_grad, up, up_bias, down, vectors):
+    rows, width = hidden.shape
+    units = up.shape[1]
+    tall = (4, rows, units)
+    return pl.pallas_call(
+        feed_forward_kernel,
+        in_specs=[WHOLE] * 8,
+        out_specs=[WHOLE] * 7,
+        out_shape=[
+            shaped(rows, width),
+            shaped(rows, width),
+            shaped(rows, width, dtype=F32),
+            shaped(width, units),
+            shaped(units, width),
+            shaped(1, units, dtype=F32),
+            shaped(8, width, dtype=F32),
+        ],
+        scratch_shapes=[
+            pltpu.VMEM((3, rows, width), BF),
+            pltpu.VMEM(tall, BF),
+            pltpu.VMEM(tall, BF),
+            pltpu.VMEM((rows, width), BF),
+            *[pltpu.VMEM((3, rows, width), BF)] * 5,
+            *[pltpu.VMEM((rows, width), F32)] * 3,
+            *transfer_sems(),
+            *transfer_sems(),
+            *transfer_sems(),
+            *transfer_sems(),
+        ],
+        name="feed_forward",
+        compiler_params=comm_params(2),
+    )(hidden, normed, inv_std, output_grad, up, up_bias, down, vectors)
+
+
+def attend_back_kernel(
+    b_ref, w_ref, e_ref, r_ref, q_ref, k_ref, v_ref, o_ref,
+    dq_ref, dk_ref, dv_ref, wg_ref,
+    land, v_aug, k_t, dks, dvs, w_total, rows_now, send, recv,
+):
+    step, last = pl.program_id(0), pl.num_programs(0) - 1
+    seq_len, block = k_ref.shape[0], q_ref.shape[0]
+    heads = k_ref.shape[1] // HD
+    pairs = heads // 2
+    gather = Gather(b_ref, land, send, recv, HALVES)
+
+    @pl.when(step == 0)
+    def _():
+        greet([mp_peer(1), mp_peer(2)])
+        repeat(HALVES, gather.start)
+        lanes = lax.broadcasted_iota(jnp.int32, (seq_len, WIDE), 1)
+        for p in range(pairs):
+            values = v_ref[:, p * WIDE : (p + 1) * WIDE].astype(F32)
+            for h in range(2):
+                other = (1 - h) * HD
+                ones = jnp.where((lanes >= other) & (lanes < other + 2), 1.0, 0.0)
+                v_aug[2 * p + h] = jnp.where(lanes // HD == h, values, ones).astype(BF)
+        k_t[...] = (k_ref[...].astype(F32) * HD**-0.5).T.astype(BF)
+        for total in (dks, dvs, w_total):
+            total[...] = jnp.zeros_like(total)
+
+    for t in range(4 * HALVES):
+
+        @pl.when(step == t)
+        def _(t=t):
+            s, j = t // HALVES, t % HALVES
+            if t == 2 * HALVES:
+                for each in range(HALVES):
+                    gather.arrive(2, each)
+            elif s in (1, 3):
+                gather.arrive(s, j)
+            rows = pl.ds(j * block, block)
+            rows_now[...] = b_ref[rows] if s == 0 else land[s - 1, rows]
+
+    branch = rows_now[...]
+    w_total[...] += mm(o_ref[...], branch, 0, 0)
+    attended_grad = mm(branch, w_ref[...], 1, 1).astype(BF).astype(F32)
+    lanes = lax.broadcasted_iota(jnp.int32, (block, WIDE), 1)
+    query_grads = []
+    for p in range(pairs):
+        wide = slice(p * WIDE, (p + 1) * WIDE)
+        inverse = jnp.concatenate(
+            [jnp.broadcast_to(r_ref[0, 2 * p + h], (HD, block)) for h in range(2)], 0
+        ).T
+        grad = (attended_grad[:, wide] * inverse).astype(BF)
+        grad_wide = grad.astype(F32)
+        product = grad_wide * o_ref[:, wide].astype(F32)
+        centered = []
+        for h in range(2):
+            other = (1 - h) * HD
+            inside = lanes // HD == h
+            row_dot = jnp.sum(jnp.where(inside, product, 0.0), -1, keepdims=True)
+            high = row_dot.astype(BF).astype(F32)
+            g_aug = jnp.where(
+                inside,
+                grad_wide,
+                jnp.where(
+                    lanes == other, -high, jnp.where(lanes == other + 1, high - row_dot, 0.0)
+                ),
+            ).astype(BF)
+            centered.append(mm(v_aug[2 * p + h], g_aug, 1, 1))
+        for h in range(2):
+            at = 2 * p + h
+            cols = slice(at * HD, (at + 1) * HD)
+            expon = e_ref[0, at]
+            score_grad = (expon.astype(F32) * centered[h]).astype(BF)
+            dvs[at] += mm(expon, grad[:, h * HD : (h + 1) * HD], 1, 0)
+            dks[at] += mm(score_grad, q_ref[:, cols], 1, 0)
+            query_grads.append(mm(k_t[cols, :], score_grad, 1, 0))
+    dq_ref[...] = jnp.concatenate(query_grads, 0).T.astype(BF)
+
+    @pl.when(step == last)
+    def _():
+        for total, out in ((dks, dk_ref), (dvs, dv_ref)):
+            out[...] = jnp.concatenate([total[h] for h in range(heads)], 1).astype(BF)
+        wg_ref[...] = w_total[...].astype(BF)
+        gather.drain()
+
+
+def attend_back(branch, out_weight, expon, inverse, q, k, v, attended):
+    rows, width = branch.shape
+    all_rows, cols = q.shape
+    block = rows // HALVES
+    heads = cols // HD
+    steps = all_rows // block
+
+    def fixed(*shape):
+        return pl.BlockSpec(shape, lambda i: (0,) * len(shape))
+
+    row_spec = pl.BlockSpec((block, cols), lambda i: (i, 0))
+    return pl.pallas_call(
+        attend_back_kernel,
+        grid=(steps,),
+        in_specs=[
+            fixed(rows, width),
+            fixed(cols, width),
+            pl.BlockSpec((1, heads, all_rows, block), lambda i: (i, 0, 0, 0)),
+            pl.BlockSpec((1, heads, 1, block), lambda i: (i, 0, 0, 0)),
+            row_spec,
+            fixed(all_rows, cols),
+            fixed(all_rows, cols),
+            row_spec,
+        ],
+        out_specs=[row_spec, fixed(all_rows, cols), fixed(all_rows, cols), fixed(cols, width)],
+        out_shape=[shaped(all_rows, cols)] * 3 + [shaped(cols, width)],
+        scratch_shapes=[
+            pltpu.VMEM((3, rows, width), BF),
+            pltpu.VMEM((heads, all_rows, WIDE), BF),
+            pltpu.VMEM((cols, all_rows), BF),
+            pltpu.VMEM((heads, all_rows, HD), F32),
+            pltpu.VMEM((heads, all_rows, HD), F32),
+            pltpu.VMEM((cols, width), F32),
+            pltpu.VMEM((block, width), BF),
+            *transfer_sems(HALVES),
+        ],
+        name="attend_back",
+        compiler_params=comm_params(3),
+    )(branch, out_weight, expon, inverse, q, k, v, attended)
+
+
+def input_back_kernel(
+    dq_ref, dk_ref, dv_ref, wq_ref, wk_ref, wv_ref, all_ref, r1_ref,
+    x_ref, qg_ref, kg_ref, vg_ref, bias_ref,
+    out, land, mine, pending, send, recv,
+):
+    rows_here = r1_ref.shape[0]
+    size = rows_here // CHUNKS
+    greet([mp_peer(1), mp_peer(2)])
+    reduce = Reduce(out, land, send, recv)
+    grads = ((dq_ref, wq_ref), (dk_ref, wk_ref), (dv_ref, wv_ref))
+
+    def part_of(starts, count):
+        total = None
+        for grad, weight in grads:
+            pieces = [grad[pl.ds(pl.multiple_of(at, size), count)] for at in starts]
+            x = pieces[0] if len(pieces) == 1 else jnp.concatenate(pieces, 0)
+            term = mm(x, weight[...], 1, 1)
+            total = term if total is None else total + term
+        return total
+
+    def chunk_rows(j):
+        return pl.ds(pl.multiple_of(j * size, size), size)
+
+    def far(j):
+        part = part_of((2 * rows_here + j * size, 3 * rows_here + j * size), size)
+        pending[chunk_rows(j)] = part[:size]
+        reduce.post(PAIR, j, part[size:])
+
+        @pl.when(j > 0)
+        def _():
+            reduce.forward_pair(j - 1, pending[chunk_rows(j - 1)])
+
+    repeat(CHUNKS, far)
+    reduce.forward_pair(CHUNKS - 1, pending[chunk_rows(CHUNKS - 1)])
+
+    def near(i):
+        part = part_of((rows_here + i * 2 * size,), 2 * size)
+        reduce.post(NEAR, 2 * i, part[:size])
+        reduce.post(NEAR, 2 * i + 1, part[size:])
+
+    repeat(2, near)
+
+    def own(i):
+        mine[pl.ds(pl.multiple_of(i * 2 * size, size), 2 * size)] = part_of((i * 2 * size,), 2 * size)
+
+    repeat(2, own)
+    tile = 256
+
+    def weights(t):
+        cols = pl.ds(pl.multiple_of(t * tile, tile), tile)
+        for (grad, _), out_ref in zip(grads, (qg_ref, kg_ref, vg_ref)):
+            total = None
+            for s in range(4):
+                term = mm(all_ref[s, :, cols], grad[pl.ds(s * rows_here, rows_here)], 0, 0)
+                total = term if total is None else total + term
+            out_ref[cols] = total.astype(BF)
+
+    repeat(all_ref.shape[2] // tile, weights)
+    bias_ref[...] = jnp.concatenate(
+        [column_sum(dq_ref[...].astype(F32)), column_sum(dv_ref[...].astype(F32))], 0
+    )
+
+    def finish(j):
+        rows = chunk_rows(j)
+        x_ref[rows] = (r1_ref[rows] + reduce.total(j, mine[rows])).astype(BF)
+
+    repeat(CHUNKS, finish)
+    reduce.drain()
+
+
+def input_back(dq, dk, dv, wq, wk, wv, gathered, resid_grad):
+    rows, width = resid_grad.shape
+    cols = dq.shape[1]
+    return pl.pallas_call(
+        input_back_kernel,
+        in_specs=[WHOLE] * 8,
+        out_specs=[WHOLE] * 5,
+        out_shape=[shaped(rows, width)] + [shaped(width, cols)] * 3 + [shaped(2, cols, dtype=F32)],
+        scratch_shapes=[
+            pltpu.VMEM((3, rows, width), BF),
+            pltpu.VMEM((3, rows, width), BF),
+            pltpu.VMEM((rows, width), F32),
+            pltpu.VMEM((rows, width), F32),
+            *transfer_sems(),
+        ],
+        name="input_back",
+        compiler_params=comm_params(4),
+    )(dq, dk, dv, wq, wk, wv, gathered, resid_grad)
+
+
+def per_device(
+    tokens, lengths, query_weight, query_bias, key_weight, value_weight, value_bias, out_weight,
+    out_bias, first_gain, first_shift, up_weight, up_bias, down_weight, down_bias, second_gain,
+    second_shift, output_grad,
+):
+    if lax.axis_size("mp") != 4 or lengths.shape[1] != 1:
+        return per_device_general(
+            tokens, lengths, query_weight, query_bias, key_weight, value_weight, value_bias,
+            out_weight, out_bias, first_gain, first_shift, up_weight, up_bias, down_weight,
+            down_bias, second_gain, second_shift, output_grad,
+        )
+    rows = tokens.shape[0]
+
+    def as_row(vector):
+        return vector.astype(F32)[None]
+
+    q, k, v, vt, gathered = gather_project(
+        tokens, query_weight, key_weight, value_weight, as_row(query_bias), as_row(value_bias)
+    )
+    relation = lax.iota(jnp.int32, 4)
+    place = jnp.bitwise_xor(relation, lax.axis_index("mp"))[:, None] * rows + lax.iota(jnp.int32, rows)
+    bias = jnp.where(place.reshape(-1, 1) < lengths[0, 0], 0.0, MASKED)
+    expon, attended, inverse, normed, inv_std, hidden = attend(
+        q, k, vt, bias, out_weight, tokens,
+        jnp.stack([out_bias, first_gain, first_shift]).astype(F32),
+    )
+    layer_out, branch, resid_grad, up_grad, down_grad, up_bias_grad, small = feed_forward(
+        hidden, normed, inv_std, output_grad, up_weight, as_row(up_bias), down_weight,
+        jnp.stack([first_gain, first_shift, down_bias, second_gain, second_shift]).astype(F32),
+    )
+    dq, dk, dv, out_grad = attend_back(branch, out_weight, expon, inverse, q, k, v, attended)
+    tokens_grad, query_grad, key_grad, value_grad, bias_grads = input_back(
+        dq, dk, dv, query_weight, key_weight, value_weight, gathered, resid_grad
+    )
+
+    def over_batches(array):
+        return lax.psum(array.astype(BF), "dp").astype(F32)
+
+    small = lax.psum(small, ("dp", "mp"))
+    return (
+        layer_out,
+        tokens_grad,
+        over_batches(query_grad),
+        over_batches(bias_grads[0]),
+        over_batches(key_grad),
+        over_batches(value_grad),
+        over_batches(bias_grads[1]),
+        over_batches(out_grad),
+        small[5],
+        small[3],
+        small[4],
+        over_batches(up_grad),
+        over_batches(up_bias_grad[0]),
+        over_batches(down_grad),
+        small[2],
+        small[0],
+        small[1],
+    )
+
+
 def solution(mesh):
     placed = (
         P(("dp", "mp"), None),

time: 739 us -> 514 us (0.70)
  waiting for transfers between devices: 421 us -> 146 us
  Pallas kernels: 75.5 us -> 261 us
  matrix products: 94.3 us -> 0 us
  other arithmetic: 35.3 us -> 18.3 us
  local copies, waits for them, and re-layouts: 24.1 us -> 9.37 us
    pallas_call x2 -> x5, Pallas kernels: 75.5 us -> 261 us  [the longest x1 102 us: feed_forward(): pl.pallas_call(feed_forward_kernel, in_specs=[WHOLE] * 8, out_specs=[WHOL...]
    reduce_scatter x4 -> x0, waiting for transfers between devices: 164 us -> none  [the longest x1 44.7 us: per_device(): lax.psum_scatter(contract_cols(lax.slice_in_dim(pre_grad, 0, local_rows *...]
    all_gather x4 -> x0, waiting for transfers between devices: 119 us -> none  [the longest x1 34.4 us: per_device(): hidden_all = lax.all_gather(hidden_low, 'mp', axis=0, tiled=True)]
    dot_general x12 -> x0, matrix products: 94.3 us -> none  [the longest x4 31.7 us: contract_cols(): lax.dot_general(left, right, (((1,), (1,)), ((), ())), preferred_element_...]
    reduce_sum x9 -> x0, other arithmetic: 14.4 us -> none  [the longest x2 4.72 us: norm_backward(): return (back, jnp.sum(grad * normed, 0), jnp.sum(grad, 0))]
    unnamed x64 -> x22, local copies, waits for them, and re-layouts: 18.5 us -> 4.57 us
    psum x1, waiting for transfers between devices: 137 us -> 146 us  [over_batches(): return lax.psum(array.astype(BF), 'dp').astype(F32)]
    convert_element_type x20 -> x12, other arithmetic: 20.8 us -> 14.5 us  [the longest x10 13.2 us: over_batches(): return lax.psum(array.astype(BF), 'dp').astype(F32)]
  transfers between devices with their start and end apart: 9 -> 1, of which waited for: 9 -> 1; matrix products, arithmetic and copies ran while one was open for 6% -> 0% of each run, Pallas kernels for 0% -> 0%
where the time goes in v2:
time: 514 us; the launch traced here: 513 us
  Pallas kernels  261 us (51%)
  waiting for transfers between devices  146 us (28%)
  blocking collectives  63.4 us (12%)
  other arithmetic  18.3 us (4%)
  between operations  14.8 us (3%)
  local copies, waits for them, and re-layouts  9.37 us (2%)
    psum x1, waiting for transfers between devices, over_batches(): return lax.psum(array.astype(BF), 'dp').astype(F32)  146 us
    pallas_call x1, Pallas kernels, feed_forward(): pl.pallas_call(feed_forward_kernel, in_specs=[WHOLE] * 8, out_specs=[WHOL...  102 us
    pallas_call x1, Pallas kernels, attend_back(): pl.pallas_call(attend_back_kernel, grid=(steps,), in_specs=[fixed(rows, w...  51.1 us
    pallas_call x1, Pallas kernels, attend(): pl.pallas_call(attend_kernel, grid=(steps,), in_specs=[pl.BlockSpec((bloc...  41.9 us
    psum x1, blocking collectives, per_device(): small = lax.psum(small, ('dp', 'mp'))  40.6 us
    pallas_call x1, Pallas kernels, gather_project(): pl.pallas_call(project_kernel, in_specs=[WHOLE] * 6, out_specs=[WHOLE] *...  33.4 us
    pallas_call x1, Pallas kernels, input_back(): pl.pallas_call(input_back_kernel, in_specs=[WHOLE] * 8, out_specs=[WHOLE]...  33.2 us
    psum x1, blocking collectives, over_batches(): return lax.psum(array.astype(BF), 'dp').astype(F32)  22.7 us
  transfers between devices with their start and end apart: 1, of which 1 were waited for; matrix products, arithmetic and copies ran while one was open for 0% of the time, Pallas kernels for 0%

profile of v2, /device:TPU:0, one launch (start us, length us, event | category | flops | bytes accessed | tf_op | source)
XLA Modules:
  0.0 513.4 jit_solution(12193280523677075500)
XLA Ops:
  7.9 1.2 broadcast_in_dim.33
  9.1 1.2 broadcast_in_dim.34
  10.3 0.7 stack.27
  11.0 0.7 stack.28
  11.7 0.7 stack.26
  12.4 1.3 broadcast_in_dim.35
  13.7 0.7 stack.30
  14.4 0.7 stack.31
  15.0 0.7 stack.32
  15.8 0.6 maximum_convert_fusion.vec_ref
  16.5 0.6 convert_element_type.51.vec_ref
  17.1 1.3 copy.37
  18.4 33.4 %gather_project.1 = (bf16[2048,256]{1,0:T(8,128)(2,1)}, bf16[2048,256]{1,0:T(8,128)(2,1)}, bf16[2048,256]{1,0:T(8,128)(2,1)}, bf16[256,2048]{1,0:T(8,128)(2,1)}, bf16[4,512,1024]{2,1,0:T(8,128)(2,1)}) custom-call(bf16[512,1024]{1,0:T(8,128)(2,1)} %x_ref.3, bf16[1024,256]{1,0:T(8,128)(2,1)} %wq_ref.3, bf16[1024,256]{1,0:T(8,128)(2,1)} %wk_ref.3, ...), custom_call_target="tpu_custom_call" | custom-call | tf_op jit(solution)/shard_map/gather_project/pallas_call | solution.py:601
  51.8 41.9 %attend.1 = (bf16[8,4,2048,256]{3,2,1,0:T(8,128)(2,1)}, bf16[2048,256]{1,0:T(8,128)(2,1)}, f32[8,4,1,256]{3,2,1,0:T(1,128)}, f32[512,1024]{1,0:T(8,128)}, f32[512,1]{1,0:T(8,128)}, /*index=5*/bf16[512,1024]{1,0:T(8,128)(2,1)}) custom-call(bf16[2048,256]{1,0:T(8,128)(2,1)} %get-tuple-element.44.q_ref, bf16[2048,256]{1,0:T(8,128)(2,1)} %get-tuple-element.45.k_ref, ...), custom_call_target="tpu_custom_call" | custom-call | tf_op jit(solution)/shard_map/attend/pallas_call | solution.py:711
  93.7 101.5 %feed_forward.1 = (bf16[512,1024]{1,0:T(8,128)(2,1)}, bf16[512,1024]{1,0:T(8,128)(2,1)}, f32[512,1024]{1,0:T(8,128)}, bf16[1024,1024]{1,0:T(8,128)(2,1)}, bf16[1...) custom-call(bf16[512,1024]{1,0:T(8,128)(2,1)} %get-tuple-element.47.h_ref, ...), custom_call_target="tpu_custom_call" | custom-call | tf_op jit(solution)/shard_map/feed_forward/pallas_call | solution.py:921
  195.2 51.1 %attend_back.1 = (bf16[2048,256]{1,0:T(8,128)(2,1)}, bf16[2048,256]{1,0:T(8,128)(2,1)}, bf16[2048,256]{1,0:T(8,128)(2,1)}, bf16[256,1024]{1,0:T(8,128)(2,1)}) custom-call(bf16[512,1024]{1,0:T(8,128)(2,1)} %get-tuple-element.51.b_ref, bf16[256,1024]{1,0:T(8,128)(2,1)} %w_ref.3, bf16[8,4,2048,256]{3,2,1,0:T(8,128)(2,1)} %get-tuple-element.52.e_ref, ...), custom_call_target="tpu_custom_call" | custom-call | tf_op jit(solution)/shard_map/attend_back/pallas_call | solution.py:1046
  246.4 33.2 %input_back.1 = (bf16[512,1024]{1,0:T(8,128)(2,1)}, bf16[1024,256]{1,0:T(8,128)(2,1)}, bf16[1024,256]{1,0:T(8,128)(2,1)}, bf16[1024,256]{1,0:T(8,128)(2,1)}, f32[2,256]{1,0:T(2,128)}) custom-call(bf16[2048,256]{1,0:T(8,128)(2,1)} %get-tuple-element.56.dq_ref, bf16[2048,256]{1,0:T(8,128)(2,1)} %get-tuple-element.57.dk_ref, ...), custom_call_target="tpu_custom_call" | custom-call | tf_op jit(solution)/shard_map/input_back/pallas_call | solution.py:1149
  279.6 0.6 copy-done.8
  280.3 22.7 %all-reduce = (bf16[256]{0:T(256)(128)(2,1)S(1)}, bf16[256]{0:T(256)(128)(2,1)S(1)}, bf16[1024]{0:T(1024)(128)(2,1)S(1)}) all-reduce(bf16[256]{0:T(256)(128)(2,1)S(1)} %get-tuple-element.72, bf16[256]{0:T(256)(128)(2,1)S(1)} %get-tuple-element.71, bf16[1024]{0:T(1024)(128)(2,1)S(1)} %convert_reduce_fusion), channel_id=1, replica_groups=mesh['dp'=8,'mp'=4] {'dp'}, use_global_device_ids=true, to_apply=%region_1.2 | all-reduce | flops 1536 | bytes 6144 | tf_op jit(solution)/shard_map/psum | solution.py:1202
  304.1 0.6 convert_element_type.63
  304.7 40.6 %psum.76 = f32[8,1024]{1,0:T(8,128)S(1)} all-reduce(f32[8,1024]{1,0:T(8,128)S(1)} %copy-done.6), channel_id=1, replica_groups=mesh['dp'=8,'mp'=4] {'dp','mp'}, use_global_device_ids=true, to_apply=%region_6.7 | all-reduce | flops 8192 | bytes 65536 | tf_op jit(solution)/shard_map/psum | solution.py:1204
  345.4 0.6 fusion
  346.0 146.4 %all-reduce.4.cloned.1.call-done = (bf16[1024,256]{1,0:T(8,128)(2,1)}, bf16[1024,256]{1,0:T(8,128)(2,1)}, bf16[1024,256]{1,0:T(8,128)(2,1)}, bf16[256,1024]{1,0:...) async-done(((bf16[1024,256]{1,0:T(8,128)(2,1)}, bf16[1024,256]{1,0:T(8,128)(2,1)}, bf16[1024,256]{1,0:T(8,128)(2,1)}, bf16[256,1024]{1,0:T(8,128)(2,1)}, ...) | async-done | bytes 6291472 | tf_op jit(solution)/shard_map/psum | solution.py:1202
  492.4 2.2 convert_element_type.52
  494.6 2.2 convert_element_type.55
  496.8 1.0 convert_element_type.56
  497.9 1.1 convert_element_type.59
  499.0 2.5 convert_element_type.60
  501.5 2.5 convert_element_type.64
  503.9 1.0 copy.47
  504.9 0.6 copy-done.3
  505.5 1.0 copy.48
  (27 shorter events, 1.4 us)
Async XLA Ops:
  7.2 485.2 %all-reduce.4.cloned.1.call-start = ((), (), s32[]{:S(2)}) async-start(), calls=%async_computation | async-start | bytes 12582912 | tf_op jit(solution)/shard_map/psum | solution.py:1202
  279.6 0.7 copy-start.8
  279.6 0.7 copy-start.7
  279.6 25.2 %copy-start.6 = (f32[8,1024]{1,0:T(8,128)S(1)}, f32[8,1024]{1,0:T(8,128)}, u32[]{:S(2)}) copy-start(f32[8,1024]{1,0:T(8,128)} %get-tuple-element.67) | copy-start | bytes 98308
  492.4 4.4 copy-start.5
  492.4 5.5 %copy-start.4 = (bf16[256,1024]{1,0:T(8,128)(2,1)S(1)}, bf16[256,1024]{1,0:T(8,128)(2,1)}, u32[]{:S(2)}) copy-start(bf16[256,1024]{1,0:T(8,128)(2,1)} %get-tuple-element.79) | copy-start | bytes 1572868
  494.6 4.4 copy-start.1
  499.0 2.5 copy-start
  501.5 2.5 copy-start.2
  503.9 1.6 copy-start.3
Sparse Core Ops, SparseCore 0:
  279.7 212.6 all-reduce.3
